TPU v7x, 128 devices: a whole 4x4x4 slice. The times are simulated.
128 devices in a mesh: batch: 8 (over y, core), vocab: 16 (over x, z).
Axes of the slice: x: 4, y: 4, z: 4, core: 2. Of those that a mesh axis runs over, the one named last changes fastest.
Arguments:
- hidden: bfloat16 [65536, 768], P(('batch', 'vocab')), may hold values from -150 to 150, as said below
- dense_w: bfloat16 [768, 768], replicated, may hold values from -0.21875 to 0.21875
- dense_b: float32 [768], replicated, may hold values from -3 to 3
- norm_gain: float32 [768], replicated, may hold values from 0.5 to 1.5
- norm_bias: float32 [768], replicated, may hold values from -2 to 2
- vocabulary_weight: bfloat16 [768, 30720], P(None, 'vocab'), may hold values from -0.21875 to 0.21875
- vocabulary_bias: bfloat16 [30720], P('vocab'), may hold values from -5 to 5
- lengths: int32 [256], P('batch'), may hold values from 32 to 256
- term_ids: int32 [256, 128], P('batch'), may hold values from -1 to 30521, as said below
Outputs:
- vectors: float32 [256, 30720], P('batch', 'vocab')
- posting_weights: float32 [128, 5, 128], P(('batch', 'vocab'))
- posting_key_codes: int32 [128, 5, 128], P(('batch', 'vocab'))
Inputs may be any that keep to these rules, and one draw needn't show every extreme that they name: `hidden`: the last encoder layer's states. `term_ids`: no term appears twice in one passage and every term is below 30522. Within the 32 passages of one batch shard, the terms t with one value of t // 1920 and one value of t % (128) number at most 5, and in every draw one owner t % (128) reaches 5 for every batch shard and every value of t // 1920.
All inputs are finite; a program needn't handle non-finite values.
Results may differ from a plain program's by a relative error of at most 0.0009.
Values may be sent and summed in bfloat16 or wider, within the bound.
A program may use at most 64 MiB of HBM per device.

v0:
```python
import math

import jax
import jax.numpy as jnp
from jax import lax
from jax.sharding import PartitionSpec as P

VOCAB = 30522
VOCAB_PADDED = 30720
L = 256
K = 128


def transform_rows(token_rows, dense_w, dense_b, norm_gain, norm_bias):
    pre = jnp.dot(token_rows, dense_w, preferred_element_type=jnp.float32) + dense_b
    activated = jax.nn.gelu(pre, approximate=False)
    centered = activated - jnp.mean(activated, axis=-1, keepdims=True)
    spread = jnp.mean(centered * centered, axis=-1, keepdims=True)
    normed = centered * lax.rsqrt(spread + 1e-06) * norm_gain + norm_bias
    return normed.astype(jnp.bfloat16)


def pool_rows(gathered, row_lengths, columns_w, columns_b, prepare):
    passages = row_lengths.shape[0]
    features = gathered.shape[1]
    width = columns_w.shape[1]
    per_block = math.gcd(passages, max(1, 512 // L))
    blocks = gathered.reshape(passages // per_block, per_block * L, features)
    block_lengths = row_lengths.reshape(passages // per_block, per_block)
    positions = jnp.arange(L, dtype=jnp.int32)
    bias_wide = columns_b.astype(jnp.float32)

    def pool_block(block_pair):
        token_rows, limits = block_pair
        normed = prepare(token_rows)
        logits = jnp.dot(normed, columns_w, preferred_element_type=jnp.float32) + bias_wide
        active = jnp.log1p(jnp.maximum(logits, 0.0)).reshape(per_block, L, width)
        counted = (positions[None, :] < limits[:, None])[:, :, None]
        return jnp.max(jnp.where(counted, active, 0.0), axis=1)

    return lax.map(pool_block, (blocks, block_lengths)).reshape(passages, width)


def local(
    hidden,
    dense_w,
    dense_b,
    norm_gain,
    norm_bias,
    vocabulary_weight,
    vocabulary_bias,
    lengths,
    term_ids,
):
    passages = lengths.shape[0]
    owner_width = vocabulary_weight.shape[1]
    vocab_count = lax.axis_size("vocab")
    batch_count = lax.axis_size("batch")
    device_list = vocab_count * batch_count
    shard_index = lax.axis_index("vocab")
    source_rows = transform_rows(hidden, dense_w, dense_b, norm_gain, norm_bias)

    def prepare(token_rows):
        return token_rows

    gathered = lax.all_gather(source_rows, "vocab", axis=0, tiled=True)
    vectors = pool_rows(gathered, lengths, vocabulary_weight, vocabulary_bias, prepare)
    column_span = shard_index * owner_width + jnp.arange(owner_width, dtype=jnp.int32)
    vectors = jnp.where(column_span[None, :] < VOCAB, vectors, 0.0)
    batch_index = lax.axis_index("batch")
    flattened_terms = term_ids.reshape(-1)
    mine = (flattened_terms >= 0) & (flattened_terms // owner_width == shard_index)
    local_columns = jnp.where(mine, flattened_terms - shard_index * owner_width, 0)
    row_index = jnp.arange(flattened_terms.shape[0], dtype=jnp.int32) // term_ids.shape[1]
    picked = vectors[row_index, local_columns]
    owners = jnp.where(mine, flattened_terms % device_list, device_list)
    onehot = (owners[:, None] == jnp.arange(device_list, dtype=jnp.int32)[None, :]).astype(
        jnp.int32
    )
    posting_slots = jnp.sum(onehot * (jnp.cumsum(onehot, axis=0) - 1), axis=1)
    capacity = 3 * passages * K // (2 * vocab_count * device_list) + 2
    overall_rows = batch_index * passages + row_index
    send_weights = (
        jnp.zeros((capacity, device_list), jnp.float32)
        .at[posting_slots, owners]
        .set(picked, mode="drop")
    )
    send_keys = (
        jnp.full((capacity, device_list), -1, jnp.int32)
        .at[posting_slots, owners]
        .set(overall_rows * VOCAB_PADDED + flattened_terms, mode="drop")
    )
    got_weights, got_keys = (
        lax.all_to_all(send_weights, ("batch", "vocab"), split_axis=1, concat_axis=1, tiled=True),
        lax.all_to_all(send_keys, ("batch", "vocab"), split_axis=1, concat_axis=1, tiled=True),
    )
    return (vectors, got_weights[None], got_keys[None])


def solution(mesh):
    in_specs = (
        P(("batch", "vocab"), None),
        P(),
        P(),
        P(),
        P(),
        P(None, "vocab"),
        P("vocab"),
        P("batch"),
        P("batch", None),
    )
    out_specs = (
        P("batch", "vocab"),
        P(("batch", "vocab"), None, None),
        P(("batch", "vocab"), None, None),
    )
    return jax.shard_map(local, mesh=mesh, in_specs=in_specs, out_specs=out_specs, check_vma=False)
```

profile of v0, /device:TPU:1, one launch (start us, length us, event | category | flops | bytes accessed | tf_op | source)
XLA Modules:
  0.0 264.2 jit_solution(16456721431749829787)
XLA Ops:
  7.2 1.2 copy-done
  8.4 5.2 %fusion.48 = (f32[512]{0:T(512)S(1)}, f32[512,768]{1,0:T(8,128)S(1)}) fusion(f32[768]{0:T(1024)} %param.13, bf16[512,768]{1,0:T(8,128)(2,1)} %param.11, bf16[768,768]{1,0:T(8,128)(2,1)S(1)} %copy-done), kind=kOutput, calls=%fused_computation.110 | convolution fusion | flops 629931520 | bytes 3544064 | tf_op jit(solution)/shard_map/dot_general | solution.py:15
  13.7 0.3 multiply_reduce_fusion
  14.0 0.3 copy-done.3
  14.4 1.2 add_convert_fusion
  15.7 0.1 copy.25
  15.8 0.6 fusion.7
  16.5 0.3 add_add_fusion
  16.7 1.2 copy.26
  18.0 1.4 fusion.6
  19.5 0.2 fusion.31
  19.7 0.1 compare_select_fusion.2
  19.8 0.1 multiply_reduce_fusion.1
  19.9 0.1 and_reduce_fusion
  20.0 15.5 %scatter_custom_fusion.1 = s32[640]{0:T(1024)S(1)} fusion(s32[4096]{0:T(1024)S(1)} %broadcast_select_fusion.1, s32[4096]{0:T(1024)S(1)} %get-tuple-element.72, s32[]{:T(128)} %constant.143.clone.1), kind=kCustom, calls=%fused_computation.104 | custom fusion | bytes 2564
  35.5 0.7 copy.29
  36.3 11.5 %all-to-all-start.1 = ((s32[5,128,1]{0,2,1:T(1,128)}), s32[5,128,1]{0,2,1:T(1,128)S(1)}, u32[]{:S(2)}, u32[]{:S(2)}) async-start(s32[5,128,1]{0,2,1:T(1,128)} %copy.29), calls=%async_computation.1 | async-start | bytes 131072 | tf_op jit(solution)/shard_map/all_to_all | solution.py:95
  47.8 0.1 reshape.326
  47.9 60.8 %all-gather.2.cloned.1.call-done = bf16[8192,768]{1,0:T(8,128)(2,1)} async-done(((bf16[512,768]{1,0:T(8,128)(2,1)}), bf16[8192,768]{1,0:T(8,128)(2,1)}) %all-gather.2.cloned.1.call-update) | async-done | bytes 12582928 | tf_op jit(solution)/shard_map/all_gather | solution.py:66
  108.7 81.1 %while.11 = (s32[]{:T(128)}, f32[16,2,1920]{2,1,0:T(2,128)S(1)}, s32[16,2]{1,0:T(8,128)S(1)}, bf16[16,512,768]{2,1,0:T(8,128)(2,1)}, bf16[768,1920]{1,0:T(8,128)(2,1)}, /*index=5*/f32[1920]{0:T(1024)S(1)}, s32[]{:T(128)}) while((s32[]{:T(128)}, f32[16,2,1920]{2,1,0:T(2,128)S(1)}, s32[16,2]{1,0:T(8,128)S(1)}, ...), condition=%wide.region_4.5_spmd.clone, body=%wide.region_2.4_spmd.clone.sunk | while | flops 1513878272 | bytes 3790957 | solution.py:41
  108.7 0.1 iota_compare_fusion.5
  108.8 4.9 %select_reduce_fusion.2 = f32[2,1920]{1,0:T(2,128)S(1)} fusion(pred[2,256]{1,0:T(4,128)(4,1)S(1)} %iota_compare_fusion.5, f32[1920]{0:T(1024)S(1)} %get-tuple-element.134, bf16[768,1920]{1,0:T(8,128)(2,1)} %get-tuple-element.133, bf16[16,512,768]{2,1,0:T(8,128)(2,1)} %get-tuple-element.132, s32[]{:T(128)} %get-tuple-element.122), kind=kOutput, calls=%fused_computation.4.clone.1 | convolution fusion | flops 1513877760 | bytes 3759616 | tf_op jit(solution)/shard_map/while/body/eval_jaxpr/dot_general | solution.py:36
  113.9 4.9 %select_reduce_fusion.2 = f32[2,1920]{1,0:T(2,128)S(1)} fusion(pred[2,256]{1,0:T(4,128)(4,1)S(1)} %iota_compare_fusion.5, f32[1920]{0:T(1024)S(1)} %get-tuple-element.134, bf16[768,1920]{1,0:T(8,128)(2,1)} %get-tuple-element.133, bf16[16,512,768]{2,1,0:T(8,128)(2,1)} %get-tuple-element.132, s32[]{:T(128)} %get-tuple-element.122), kind=kOutput, calls=%fused_computation.4.clone.1 | convolution fusion | flops 1513877760 | bytes 3759616 | tf_op jit(solution)/shard_map/while/body/eval_jaxpr/dot_general | solution.py:36
  118.9 0.1 iota_compare_fusion.5
  119.0 4.9 %select_reduce_fusion.2 = f32[2,1920]{1,0:T(2,128)S(1)} fusion(pred[2,256]{1,0:T(4,128)(4,1)S(1)} %iota_compare_fusion.5, f32[1920]{0:T(1024)S(1)} %get-tuple-element.134, bf16[768,1920]{1,0:T(8,128)(2,1)} %get-tuple-element.133, bf16[16,512,768]{2,1,0:T(8,128)(2,1)} %get-tuple-element.132, s32[]{:T(128)} %get-tuple-element.122), kind=kOutput, calls=%fused_computation.4.clone.1 | convolution fusion | flops 1513877760 | bytes 3759616 | tf_op jit(solution)/shard_map/while/body/eval_jaxpr/dot_general | solution.py:36
  124.0 4.9 %select_reduce_fusion.2 = f32[2,1920]{1,0:T(2,128)S(1)} fusion(pred[2,256]{1,0:T(4,128)(4,1)S(1)} %iota_compare_fusion.5, f32[1920]{0:T(1024)S(1)} %get-tuple-element.134, bf16[768,1920]{1,0:T(8,128)(2,1)} %get-tuple-element.133, bf16[16,512,768]{2,1,0:T(8,128)(2,1)} %get-tuple-element.132, s32[]{:T(128)} %get-tuple-element.122), kind=kOutput, calls=%fused_computation.4.clone.1 | convolution fusion | flops 1513877760 | bytes 3759616 | tf_op jit(solution)/shard_map/while/body/eval_jaxpr/dot_general | solution.py:36
  129.0 0.1 iota_compare_fusion.5
  129.1 4.9 %select_reduce_fusion.2 = f32[2,1920]{1,0:T(2,128)S(1)} fusion(pred[2,256]{1,0:T(4,128)(4,1)S(1)} %iota_compare_fusion.5, f32[1920]{0:T(1024)S(1)} %get-tuple-element.134, bf16[768,1920]{1,0:T(8,128)(2,1)} %get-tuple-element.133, bf16[16,512,768]{2,1,0:T(8,128)(2,1)} %get-tuple-element.132, s32[]{:T(128)} %get-tuple-element.122), kind=kOutput, calls=%fused_computation.4.clone.1 | convolution fusion | flops 1513877760 | bytes 3759616 | tf_op jit(solution)/shard_map/while/body/eval_jaxpr/dot_general | solution.py:36
  134.1 0.1 iota_compare_fusion.5
  134.1 4.9 %select_reduce_fusion.2 = f32[2,1920]{1,0:T(2,128)S(1)} fusion(pred[2,256]{1,0:T(4,128)(4,1)S(1)} %iota_compare_fusion.5, f32[1920]{0:T(1024)S(1)} %get-tuple-element.134, bf16[768,1920]{1,0:T(8,128)(2,1)} %get-tuple-element.133, bf16[16,512,768]{2,1,0:T(8,128)(2,1)} %get-tuple-element.132, s32[]{:T(128)} %get-tuple-element.122), kind=kOutput, calls=%fused_computation.4.clone.1 | convolution fusion | flops 1513877760 | bytes 3759616 | tf_op jit(solution)/shard_map/while/body/eval_jaxpr/dot_general | solution.py:36
  139.2 4.9 %select_reduce_fusion.2 = f32[2,1920]{1,0:T(2,128)S(1)} fusion(pred[2,256]{1,0:T(4,128)(4,1)S(1)} %iota_compare_fusion.5, f32[1920]{0:T(1024)S(1)} %get-tuple-element.134, bf16[768,1920]{1,0:T(8,128)(2,1)} %get-tuple-element.133, bf16[16,512,768]{2,1,0:T(8,128)(2,1)} %get-tuple-element.132, s32[]{:T(128)} %get-tuple-element.122), kind=kOutput, calls=%fused_computation.4.clone.1 | convolution fusion | flops 1513877760 | bytes 3759616 | tf_op jit(solution)/shard_map/while/body/eval_jaxpr/dot_general | solution.py:36
  144.3 4.9 %select_reduce_fusion.2 = f32[2,1920]{1,0:T(2,128)S(1)} fusion(pred[2,256]{1,0:T(4,128)(4,1)S(1)} %iota_compare_fusion.5, f32[1920]{0:T(1024)S(1)} %get-tuple-element.134, bf16[768,1920]{1,0:T(8,128)(2,1)} %get-tuple-element.133, bf16[16,512,768]{2,1,0:T(8,128)(2,1)} %get-tuple-element.132, s32[]{:T(128)} %get-tuple-element.122), kind=kOutput, calls=%fused_computation.4.clone.1 | convolution fusion | flops 1513877760 | bytes 3759616 | tf_op jit(solution)/shard_map/while/body/eval_jaxpr/dot_general | solution.py:36
  149.4 4.9 %select_reduce_fusion.2 = f32[2,1920]{1,0:T(2,128)S(1)} fusion(pred[2,256]{1,0:T(4,128)(4,1)S(1)} %iota_compare_fusion.5, f32[1920]{0:T(1024)S(1)} %get-tuple-element.134, bf16[768,1920]{1,0:T(8,128)(2,1)} %get-tuple-element.133, bf16[16,512,768]{2,1,0:T(8,128)(2,1)} %get-tuple-element.132, s32[]{:T(128)} %get-tuple-element.122), kind=kOutput, calls=%fused_computation.4.clone.1 | convolution fusion | flops 1513877760 | bytes 3759616 | tf_op jit(solution)/shard_map/while/body/eval_jaxpr/dot_general | solution.py:36
  154.4 4.9 %select_reduce_fusion.2 = f32[2,1920]{1,0:T(2,128)S(1)} fusion(pred[2,256]{1,0:T(4,128)(4,1)S(1)} %iota_compare_fusion.5, f32[1920]{0:T(1024)S(1)} %get-tuple-element.134, bf16[768,1920]{1,0:T(8,128)(2,1)} %get-tuple-element.133, bf16[16,512,768]{2,1,0:T(8,128)(2,1)} %get-tuple-element.132, s32[]{:T(128)} %get-tuple-element.122), kind=kOutput, calls=%fused_computation.4.clone.1 | convolution fusion | flops 1513877760 | bytes 3759616 | tf_op jit(solution)/shard_map/while/body/eval_jaxpr/dot_general | solution.py:36
  159.5 4.9 %select_reduce_fusion.2 = f32[2,1920]{1,0:T(2,128)S(1)} fusion(pred[2,256]{1,0:T(4,128)(4,1)S(1)} %iota_compare_fusion.5, f32[1920]{0:T(1024)S(1)} %get-tuple-element.134, bf16[768,1920]{1,0:T(8,128)(2,1)} %get-tuple-element.133, bf16[16,512,768]{2,1,0:T(8,128)(2,1)} %get-tuple-element.132, s32[]{:T(128)} %get-tuple-element.122), kind=kOutput, calls=%fused_computation.4.clone.1 | convolution fusion | flops 1513877760 | bytes 3759616 | tf_op jit(solution)/shard_map/while/body/eval_jaxpr/dot_general | solution.py:36
  164.6 4.9 %select_reduce_fusion.2 = f32[2,1920]{1,0:T(2,128)S(1)} fusion(pred[2,256]{1,0:T(4,128)(4,1)S(1)} %iota_compare_fusion.5, f32[1920]{0:T(1024)S(1)} %get-tuple-element.134, bf16[768,1920]{1,0:T(8,128)(2,1)} %get-tuple-element.133, bf16[16,512,768]{2,1,0:T(8,128)(2,1)} %get-tuple-element.132, s32[]{:T(128)} %get-tuple-element.122), kind=kOutput, calls=%fused_computation.4.clone.1 | convolution fusion | flops 1513877760 | bytes 3759616 | tf_op jit(solution)/shard_map/while/body/eval_jaxpr/dot_general | solution.py:36
  169.6 4.9 %select_reduce_fusion.2 = f32[2,1920]{1,0:T(2,128)S(1)} fusion(pred[2,256]{1,0:T(4,128)(4,1)S(1)} %iota_compare_fusion.5, f32[1920]{0:T(1024)S(1)} %get-tuple-element.134, bf16[768,1920]{1,0:T(8,128)(2,1)} %get-tuple-element.133, bf16[16,512,768]{2,1,0:T(8,128)(2,1)} %get-tuple-element.132, s32[]{:T(128)} %get-tuple-element.122), kind=kOutput, calls=%fused_computation.4.clone.1 | convolution fusion | flops 1513877760 | bytes 3759616 | tf_op jit(solution)/shard_map/while/body/eval_jaxpr/dot_general | solution.py:36
  174.7 4.9 %select_reduce_fusion.2 = f32[2,1920]{1,0:T(2,128)S(1)} fusion(pred[2,256]{1,0:T(4,128)(4,1)S(1)} %iota_compare_fusion.5, f32[1920]{0:T(1024)S(1)} %get-tuple-element.134, bf16[768,1920]{1,0:T(8,128)(2,1)} %get-tuple-element.133, bf16[16,512,768]{2,1,0:T(8,128)(2,1)} %get-tuple-element.132, s32[]{:T(128)} %get-tuple-element.122), kind=kOutput, calls=%fused_computation.4.clone.1 | convolution fusion | flops 1513877760 | bytes 3759616 | tf_op jit(solution)/shard_map/while/body/eval_jaxpr/dot_general | solution.py:36
  179.8 4.9 %select_reduce_fusion.2 = f32[2,1920]{1,0:T(2,128)S(1)} fusion(pred[2,256]{1,0:T(4,128)(4,1)S(1)} %iota_compare_fusion.5, f32[1920]{0:T(1024)S(1)} %get-tuple-element.134, bf16[768,1920]{1,0:T(8,128)(2,1)} %get-tuple-element.133, bf16[16,512,768]{2,1,0:T(8,128)(2,1)} %get-tuple-element.132, s32[]{:T(128)} %get-tuple-element.122), kind=kOutput, calls=%fused_computation.4.clone.1 | convolution fusion | flops 1513877760 | bytes 3759616 | tf_op jit(solution)/shard_map/while/body/eval_jaxpr/dot_general | solution.py:36
  184.8 4.9 %select_reduce_fusion.2 = f32[2,1920]{1,0:T(2,128)S(1)} fusion(pred[2,256]{1,0:T(4,128)(4,1)S(1)} %iota_compare_fusion.5, f32[1920]{0:T(1024)S(1)} %get-tuple-element.134, bf16[768,1920]{1,0:T(8,128)(2,1)} %get-tuple-element.133, bf16[16,512,768]{2,1,0:T(8,128)(2,1)} %get-tuple-element.132, s32[]{:T(128)} %get-tuple-element.122), kind=kOutput, calls=%fused_computation.4.clone.1 | convolution fusion | flops 1513877760 | bytes 3759616 | tf_op jit(solution)/shard_map/while/body/eval_jaxpr/dot_general | solution.py:36
  189.8 0.2 reshape.328
  190.0 32.8 %gather_fusion = f32[4096]{0:T(1024)S(1)} fusion(f32[32,1920]{1,0:T(8,128)S(1)} %broadcast_select_fusion, s32[4096]{0:T(1024)S(1)} %bitcast.71), kind=kCustom, calls=%fused_computation | custom fusion | bytes 65536 | tf_op jit(solution)/shard_map/gather | solution.py:75
  222.9 15.5 %scatter_custom_fusion = f32[640]{0:T(1024)S(1)} fusion(s32[4096]{0:T(1024)S(1)} %broadcast_select_fusion.1, f32[4096]{0:T(1024)S(1)} %gather_fusion, f32[]{:T(128)} %constant.38.clone.1), kind=kCustom, calls=%fused_computation.106 | custom fusion | bytes 2564
  238.4 0.7 copy.27
  239.1 8.0 %all-to-all-start = ((f32[5,128,1]{0,2,1:T(1,128)}), f32[5,128,1]{0,2,1:T(1,128)S(1)}, u32[]{:S(2)}, u32[]{:S(2)}) async-start(f32[5,128,1]{0,2,1:T(1,128)} %copy.27), calls=%async_computation | async-start | bytes 131072 | tf_op jit(solution)/shard_map/all_to_all | solution.py:94
  247.2 0.7 copy.30
  247.8 8.9 %all-to-all-done = f32[5,128,1]{0,2,1:T(1,128)S(1)} async-done(((f32[5,128,1]{0,2,1:T(1,128)}), f32[5,128,1]{0,2,1:T(1,128)S(1)}, u32[]{:S(2)}, u32[]{:S(2)}) %all-to-all-start) | async-done | bytes 2592 | tf_op jit(solution)/shard_map/all_to_all | solution.py:94
  256.7 0.7 copy.28
  (75 shorter events, 1.5 us)
Async XLA Ops:
  7.2 1.3 copy-start
  7.2 101.6 %all-gather.2.cloned.1.call-start = ((), (), s32[]{:S(2)}) async-start(), calls=%async_computation.2 | async-start | bytes 13369344 | tf_op jit(solution)/shard_map/all_gather | solution.py:66
  13.7 0.7 copy-start.3
  13.7 0.7 copy-start.4
  14.4 1.3 copy-start.2
  18.0 1.8 copy-start.7
  18.0 1.9 copy-start.6
  18.0 29.8 %copy-start.5 = (bf16[1920]{0:T(1024)(128)(2,1)S(1)}, bf16[1920]{0:T(1024)(128)(2,1)}, u32[]{:S(2)}) copy-start(bf16[1920]{0:T(1024)(128)(2,1)} %param.17) | copy-start | bytes 11524
  18.0 29.8 %copy-start.8 = (s32[32]{0:T(128)S(1)}, s32[32]{0:T(128)}, u32[]{:S(2)}) copy-start(s32[32]{0:T(128)} %param.18) | copy-start | bytes 388
  36.3 202.9 %all-to-all-start.1 = ((s32[5,128,1]{0,2,1:T(1,128)}), s32[5,128,1]{0,2,1:T(1,128)S(1)}, u32[]{:S(2)}, u32[]{:S(2)}) async-start(s32[5,128,1]{0,2,1:T(1,128)} %copy.29), calls=%async_computation.1 | async-start | bytes 131072 | tf_op jit(solution)/shard_map/all_to_all | solution.py:95
  190.0 32.9 %copy-start.1 = (f32[32,1920]{1,0:T(8,128)}, f32[32,1920]{1,0:T(8,128)S(1)}, u32[]{:S(2)}) copy-start(f32[32,1920]{1,0:T(8,128)S(1)} %broadcast_select_fusion) | copy-start | bytes 737284
  239.1 17.6 %all-to-all-start = ((f32[5,128,1]{0,2,1:T(1,128)}), f32[5,128,1]{0,2,1:T(1,128)S(1)}, u32[]{:S(2)}, u32[]{:S(2)}) async-start(f32[5,128,1]{0,2,1:T(1,128)} %copy.27), calls=%async_computation | async-start | bytes 131072 | tf_op jit(solution)/shard_map/all_to_all | solution.py:94
Sparse Core Ops, SparseCore 0:
  15.8 92.9 all-gather.1
where the time goes:
time: 265 us; the launch traced here: 264 us
  matrix products  84.2 us (32%)
  local copies, waits for them, and re-layouts  70.2 us (26%)
  waiting for transfers between devices  69.7 us (26%)
  starting transfers between devices  19.6 us (7%)
  between operations  14.3 us (5%)
  other arithmetic  5.67 us (2%)
    dot_general x16, matrix products, pool_block(): jnp.dot(normed, columns_w, preferred_element_type=jnp.float32) + bias_wide  79 us
    all_gather x1, waiting for transfers between devices, local(): gathered = lax.all_gather(source_rows, 'vocab', axis=0, tiled=True)  60.8 us
    gather x1, local copies, waits for them, and re-layouts, local(): picked = vectors[row_index, local_columns]  32.8 us
    unnamed x20, local copies, waits for them, and re-layouts  32.6 us
    all_to_all x1, starting transfers between devices, local(): lax.all_to_all(send_keys, ('batch', 'vocab'), split_axis=1, concat_axis=1...  11.5 us
    all_to_all x1, waiting for transfers between devices, local(): lax.all_to_all(send_weights, ('batch', 'vocab'), split_axis=1, concat_axi...  8.9 us
    all_to_all x1, starting transfers between devices, local(): lax.all_to_all(send_weights, ('batch', 'vocab'), split_axis=1, concat_axi...  8.04 us
  transfers between devices with their start and end apart: 3, of which 2 were waited for; matrix products, arithmetic and copies ran while one was open for 57% of the time, Pallas kernels for 0%

commit v1 on v0

v1 whole, which is shorter than its diff:
```python
import functools

import jax
import jax.numpy as jnp
from jax import lax
from jax.experimental import pallas as pl
from jax.experimental.pallas import tpu as pltpu
from jax.sharding import PartitionSpec as P

VOCAB = 30522
VOCAB_PADDED = 30720
L = 256
K = 128
LIMIT = 5
LANES = 128
BIG = 1 << 20


def transform_kernel(lengths_ref, hidden_ref, w_ref, b_ref, gain_ref, bias_ref, out_ref):
    pre = jnp.dot(hidden_ref[...], w_ref[...], preferred_element_type=jnp.float32) + b_ref[...]
    act = 0.5 * pre * (1.0 + lax.erf(pre * (0.5 ** 0.5)))
    centered = act - jnp.mean(act, axis=-1, keepdims=True)
    spread = jnp.mean(centered * centered, axis=-1, keepdims=True)
    normed = centered * lax.rsqrt(spread + 1e-06) * gain_ref[...] + bias_ref[...]
    places = lax.broadcasted_iota(jnp.int32, normed.shape, 0)
    limit = lengths_ref[pl.program_id(0)]
    normed = jnp.where(places < limit, normed, normed[0:1, :])
    out_ref[...] = normed.astype(jnp.bfloat16)


def transform(hidden, lengths2, dense_w, dense_b, norm_gain, norm_bias):
    rows, width = hidden.shape
    vec = pl.BlockSpec((1, width), lambda i, *_: (0, 0))
    return pl.pallas_call(
        transform_kernel,
        grid_spec=pltpu.PrefetchScalarGridSpec(
            num_scalar_prefetch=1,
            grid=(rows // L,),
            in_specs=[
                pl.BlockSpec((L, width), lambda i, *_: (i, 0)),
                pl.BlockSpec((width, width), lambda i, *_: (0, 0)),
                vec, vec, vec,
            ],
            out_specs=pl.BlockSpec((L, width), lambda i, *_: (i, 0)),
        ),
        out_shape=jax.ShapeDtypeStruct((rows, width), jnp.bfloat16),
    )(lengths2, hidden, dense_w, dense_b[None], norm_gain[None], norm_bias[None])


def pool_kernel(s_ref, w_ref, bias_ref, first_ref, out_ref, tops):
    passages = s_ref.shape[0] // L
    width = w_ref.shape[1]
    step = 640

    def body(n, _):
        c = pl.multiple_of(n * step, LANES)
        for r in range(passages):
            d = jnp.dot(s_ref[r * L:(r + 1) * L, :], w_ref[:, pl.ds(c, step)], preferred_element_type=jnp.float32)
            tops[r, :, pl.ds(c, step)] = jnp.max(d.reshape(L // 8, 8, step), axis=0)
        return 0

    lax.fori_loop(0, width // step, body, 0)
    best = jnp.max(tops[...], axis=1) + bias_ref[...].astype(jnp.float32)
    columns = first_ref[0] + lax.broadcasted_iota(jnp.int32, best.shape, 1)
    out_ref[...] = jnp.where(columns < VOCAB, jnp.log1p(jnp.maximum(best, 0.0)), 0.0)


def pool(gathered, columns_w, columns_b, first):
    rows, features = gathered.shape
    width = columns_w.shape[1]
    passages = rows // L
    per = 8
    return pl.pallas_call(
        pool_kernel,
        grid=(passages // per,),
        in_specs=[
            pl.BlockSpec((per * L, features), lambda i: (i, 0)),
            pl.BlockSpec((features, width), lambda i: (0, 0)),
            pl.BlockSpec((1, width), lambda i: (0, 0)),
            pl.BlockSpec(memory_space=pltpu.SMEM),
        ],
        out_specs=pl.BlockSpec((per, width), lambda i: (i, 0)),
        scratch_shapes=[pltpu.VMEM((per, 8, width), jnp.float32)],
        out_shape=jax.ShapeDtypeStruct((passages, width), jnp.float32),
        compiler_params=pltpu.CompilerParams(vmem_limit_bytes=48 * 2**20),
    )(gathered, columns_w, columns_b[None], first)


def pick_kernel(where_ref, terms_ref, vectors_ref, out_ref, codes):
    passages, places = terms_ref.shape
    first, first_passage = where_ref[0], where_ref[1]
    groups = vectors_ref.shape[1] // LANES
    out_ref[...] = jnp.zeros_like(out_ref)
    k_row = (lax.broadcasted_iota(jnp.int32, (1, places), 1) + 1).astype(jnp.float32)
    j_col = lax.broadcasted_iota(jnp.int32, (16, places), 0)
    o_col = lax.broadcasted_iota(jnp.int32, (LANES, places), 0)
    for p in range(passages):
        t = terms_ref[p:p + 1, :]
        rel = t - first
        j = jnp.where((t >= 0) & (rel >= 0), rel // LANES, 99)
        a = jnp.where(j_col == j, k_row, 0.0).astype(jnp.bfloat16)
        b = jnp.where(o_col == t % LANES, 1.0, 0.0).astype(jnp.bfloat16)
        found = lax.dot_general(a, b, (((1,), (1,)), ((), ())), preferred_element_type=jnp.float32)
        found = found.astype(jnp.int32)
        codes[:, p, :] = jnp.where(found > 0, p * places + found - 1, BIG)
    last = jnp.full((1, LANES), -1, jnp.int32)
    lane = lax.broadcasted_iota(jnp.int32, (passages, LANES), 1)
    row = lax.broadcasted_iota(jnp.int32, (passages, LANES), 0)
    for c in range(LIMIT):
        low = jnp.full((passages, LANES), BIG, jnp.int32)
        for j in range(groups):
            code = codes[j]
            low = jnp.minimum(low, jnp.where(code > last, code, BIG))
        low = jnp.min(low, axis=0, keepdims=True)
        weight = jnp.zeros((passages, LANES), jnp.float32)
        key = jnp.zeros((passages, LANES), jnp.int32)
        for j in range(groups):
            hit = (codes[j] == low) & (low < BIG)
            weight = weight + jnp.where(hit, vectors_ref[:, j * LANES:(j + 1) * LANES], 0.0)
            key = key + jnp.where(hit, (first_passage + row) * VOCAB_PADDED + first + j * LANES + lane + 1, 0)
        out_ref[c:c + 1, :] = jnp.sum(weight, axis=0, keepdims=True)
        out_ref[8 + c:9 + c, :] = (jnp.sum(key, axis=0, keepdims=True) - 1).astype(jnp.float32)
        last = low


def pick(term_ids, vectors, first, first_passage):
    where = jnp.stack([first, first_passage]).astype(jnp.int32)
    return pl.pallas_call(
        pick_kernel,
        in_specs=[pl.BlockSpec(memory_space=pltpu.SMEM)] + [pl.BlockSpec(memory_space=pltpu.VMEM)] * 2,
        out_specs=pl.BlockSpec(memory_space=pltpu.VMEM),
        scratch_shapes=[pltpu.VMEM((16,) + term_ids.shape, jnp.int32)],
        out_shape=jax.ShapeDtypeStruct((16, LANES), jnp.float32),
    )(where, term_ids, vectors)


def local(hidden, dense_w, dense_b, norm_gain, norm_bias, vocabulary_weight, vocabulary_bias, lengths, term_ids):
    passages = lengths.shape[0]
    width = vocabulary_weight.shape[1]
    v = lax.axis_index("vocab")
    b = lax.axis_index("batch")
    own = hidden.shape[0] // L
    mine = lax.dynamic_slice(lengths, (v * own,), (own,))
    states = transform(hidden, mine, dense_w, dense_b, norm_gain, norm_bias)
    gathered = lax.all_gather(states, "vocab", axis=0, tiled=True)
    first = v * width
    vectors = pool(gathered, vocabulary_weight, vocabulary_bias, first[None].astype(jnp.int32))
    sent = pick(term_ids, vectors, first, b * passages)
    got = lax.all_to_all(sent, ("batch", "vocab"), split_axis=1, concat_axis=1, tiled=True)
    return vectors, got[None, :LIMIT], got[None, 8:8 + LIMIT].astype(jnp.int32)


def solution(mesh):
    in_specs = (
        P(("batch", "vocab"), None), P(), P(), P(), P(),
        P(None, "vocab"), P("vocab"), P("batch"), P("batch", None),
    )
    out_specs = (P("batch", "vocab"), P(("batch", "vocab"), None, None), P(("batch", "vocab"), None, None))
    return jax.shard_map(local, mesh=mesh, in_specs=in_specs, out_specs=out_specs, check_vma=False)
```

time: 265 us -> 175 us (0.66)
  matrix products: 84.2 us -> 0 us
  local copies, waits for them, and re-layouts: 70.2 us -> 7.33 us
  Pallas kernels: 0 us -> 42.5 us
  waiting for transfers between devices: 69.7 us -> 92.5 us
  starting transfers between devices: 19.6 us -> 0.04 us
  blocking collectives: 0 us -> 17.4 us
  other arithmetic: 5.67 us -> 0.8 us
    dot_general x17 -> x0, matrix products: 84.2 us -> none  [the longest x16 79 us: pool_block(): jnp.dot(normed, columns_w, preferred_element_type=jnp.float32) + bias_wide]
    pallas_call x0 -> x3, Pallas kernels: none -> 42.5 us  [the longest x1 35.2 us: pool(): pl.pallas_call(pool_kernel, grid=(passages // per,), in_specs=[pl.BlockSp...]
    gather x1 -> x0, local copies, waits for them, and re-layouts: 32.8 us -> none  [local(): picked = vectors[row_index, local_columns]]
    all_gather x1, waiting for transfers between devices: 60.8 us -> 92.5 us  [local(): gathered = lax.all_gather(states, 'vocab', axis=0, tiled=True)]
    unnamed x20 -> x6, local copies, waits for them, and re-layouts: 32.6 us -> 1.31 us
    all_to_all x2 -> x0, starting transfers between devices: 19.5 us -> none  [the longest x1 11.5 us: local(): lax.all_to_all(send_keys, ('batch', 'vocab'), split_axis=1, concat_axis=1...]
    all_to_all x0 -> x1, blocking collectives: none -> 17.4 us  [local(): lax.all_to_all(sent, ('batch', 'vocab'), split_axis=1, concat_axis=1, til...]
    all_to_all x2 -> x0, waiting for transfers between devices: 8.91 us -> none  [the longest x1 8.9 us: local(): lax.all_to_all(send_weights, ('batch', 'vocab'), split_axis=1, concat_axi...]
  transfers between devices with their start and end apart: 3 -> 1, of which waited for: 2 -> 1; matrix products, arithmetic and copies ran while one was open for 57% -> 0% of each run, Pallas kernels for 0% -> 0%
where the time goes in v1:
time: 175 us
  waiting for transfers between devices  92.5 us (53%)
  Pallas kernels  42.5 us (24%)
  blocking collectives  17.4 us (10%)
  between operations  14.1 us (8%)
  local copies, waits for them, and re-layouts  7.33 us (4%)
    all_gather x1, waiting for transfers between devices, local(): gathered = lax.all_gather(states, 'vocab', axis=0, tiled=True)  92.5 us
    pallas_call x1, Pallas kernels, pool(): pl.pallas_call(pool_kernel, grid=(passages // per,), in_specs=[pl.BlockSp...  35.2 us
    all_to_all x1, blocking collectives, local(): lax.all_to_all(sent, ('batch', 'vocab'), split_axis=1, concat_axis=1, til...  17.4 us
    pallas_call x1, Pallas kernels, transform(): pl.pallas_call(transform_kernel, grid_spec=pltpu.PrefetchScalarGridSpec(n...  4.48 us
  transfers between devices with their start and end apart: 1, of which 1 were waited for; matrix products, arithmetic and copies ran while one was open for 0% of the time, Pallas kernels for 0%

profile of v1, /device:TPU:1, one launch (start us, length us, event | category | flops | bytes accessed | tf_op | source)
XLA Modules:
  0.0 174.7 jit_solution(10884260404953567074)
XLA Ops:
  7.2 0.0 copy-start.1
  7.2 0.0 copy-start
  7.2 0.0 all-gather.2.cloned.1.call-start
  7.2 1.4 broadcast_in_dim.19.b_ref
  8.7 1.3 broadcast_in_dim.20.gain_ref
  9.9 1.3 broadcast_in_dim.21.bias_ref
  11.2 1.2 dynamic_slice.3.lengths_ref
  12.5 4.5 %shard_map.112 = bf16[512,768]{1,0:T(8,128)(2,1)} custom-call(s32[2]{0:T(128)} %dynamic_slice.3.lengths_ref, bf16[512,768]{1,0:T(8,128)(2,1)} %hidden_ref.1, bf16[768,768]{1,0:T(8,128)(2,1)} %w_ref.2, f32[1,768]{1,0:T(1,128)} %broadcast_in_dim.19.b_ref, f32[1,768]{1,0:T(1,128)} %broadcast_in_dim.20.gain_ref, f32[1,768]{1,0:T(1,128)} %broadcast_in_dim.21.bias_ref), custom_call_target="tpu_custom_call" | custom-call | tf_op jit(solution)/shard_map/pallas_call | solution.py:34
  16.9 0.0 all-gather.2.cloned.1.call-update
  17.0 0.0 copy-done.1
  17.0 0.6 pad_add_fusion.where_ref
  17.6 92.5 %all-gather.2.cloned.1.call-done.s_ref = bf16[8192,768]{1,0:T(8,128)(2,1)} async-done(((bf16[512,768]{1,0:T(8,128)(2,1)}), bf16[8192,768]{1,0:T(8,128)(2,1)}) %all-gather.2.cloned.1.call-update) | async-done | bytes 12582928 | tf_op jit(solution)/shard_map/all_gather | solution.py:145
  110.1 0.0 copy-done
  110.1 35.2 %shard_map.113.vectors_ref = f32[32,1920]{1,0:T(8,128)} custom-call(bf16[8192,768]{1,0:T(8,128)(2,1)} %all-gather.2.cloned.1.call-done.s_ref, bf16[768,1920]{1,0:T(8,128)(2,1)S(1)} %copy-done, bf16[1,1920]{1,0:T(2,128)(2,1)S(1)} %broadcast_in_dim.22.bias_ref, s32[1]{0:T(128)} %bitcast.first_ref), custom_call_target="tpu_custom_call" | custom-call | tf_op jit(solution)/shard_map/pallas_call | solution.py:73
  145.2 2.9 %shard_map.114 = f32[16,128]{1,0:T(8,128)} custom-call(s32[2]{0:T(128)} %pad_add_fusion.where_ref, s32[32,128]{1,0:T(8,128)} %terms_ref.1, f32[32,1920]{1,0:T(8,128)} %shard_map.113.vectors_ref), custom_call_target="tpu_custom_call" | custom-call | tf_op jit(solution)/shard_map/pallas_call | solution.py:128
  148.1 0.8 copy.14
  148.9 17.4 %all_to_all.9 = f32[16,128,1]{0,2,1:T(1,128)S(1)} all-to-all(f32[16,128,1]{0,2,1:T(1,128)S(1)} %copy.14), channel_id=1, replica_groups=mesh['batch'=8,'vocab'=16] {'batch','vocab'}, dimensions={1} | all-to-all | bytes 16384 | tf_op jit(solution)/shard_map/all_to_all | solution.py:149
  166.3 0.2 slice_convert_fusion
  166.5 0.7 copy.15
  167.2 0.7 copy.16
  (1 shorter events, 0.0 us)
Async XLA Ops:
  7.2 9.8 %copy-start.1 = (bf16[1920]{0:T(1024)(128)(2,1)S(1)}, bf16[1920]{0:T(1024)(128)(2,1)}, u32[]{:S(2)}) copy-start(bf16[1920]{0:T(1024)(128)(2,1)} %param.15) | copy-start | bytes 11524
  7.2 102.9 %copy-start = (bf16[768,1920]{1,0:T(8,128)(2,1)S(1)}, bf16[768,1920]{1,0:T(8,128)(2,1)}, u32[]{:S(2)}) copy-start(bf16[768,1920]{1,0:T(8,128)(2,1)} %w_ref.3) | copy-start | bytes 8847364
  7.2 102.9 %all-gather.2.cloned.1.call-start = ((), (), s32[]{:S(2)}) async-start(), calls=%async_computation.1 | async-start | bytes 13369344 | tf_op jit(solution)/shard_map/all_gather | solution.py:145
Sparse Core Ops, SparseCore 0:
  17.1 92.9 all-gather.1

commit v2 on v1

v2 whole, which is shorter than its diff:
```python
import jax
import jax.numpy as jnp
from jax import lax
from jax.experimental import pallas as pl
from jax.experimental.pallas import tpu as pltpu
from jax.sharding import PartitionSpec as P

VOCAB = 30522
VOCAB_PADDED = 30720
L = 256
K = 128
LIMIT = 5
LANES = 128
BIG = 1 << 20


MESH = pl.DeviceIdType.MESH
WIDE = 1024
PIECE = 512
DIRECT = 320
SLICE = 112
DELTA = (0, -1, 1, 2)
ORDER = (
    (0, 0),
    (1, 0), (0, 1), (1, 1),
    (2, 0), (2, 1), (0, 2), (1, 2), (2, 2),
    (3, 0), (3, 1), (3, 2), (0, 3), (1, 3), (2, 3), (3, 3),
)


def encode_kernel(
    lengths_ref, hidden_ref, dense_ref, b_ref, gain_ref, bias_ref, weight_ref, vbias_ref, out_ref,
    hid, den, states, weights, tops, pooled, landed, local_sem, send_sem, recv_sem,
):
    b, v = lax.axis_index("batch"), lax.axis_index("vocab")
    y, c = b // 2, b % 2
    x, z = v // 4, v % 4
    sign = 1 - 2 * c

    def device(dx=0, dy=0, dz=0, flip=0):
        core = 1 - c if flip else c
        return (2 * ((y + dy + 4) % 4) + core, 4 * ((x + dx + 4) % 4) + (z + dz + 4) % 4)

    def send(index, source, target, to):
        copy = pltpu.make_async_remote_copy(
            src_ref=source, dst_ref=target, send_sem=send_sem.at[index], recv_sem=recv_sem.at[index],
            device_id=to, device_id_type=MESH,
        )
        copy.start()

    def got(index, region):
        pltpu.make_async_remote_copy(
            src_ref=region, dst_ref=region, send_sem=send_sem.at[index], recv_sem=recv_sem.at[index],
            device_id=device(flip=1), device_id_type=MESH,
        ).wait_recv()

    def left(index, region):
        pltpu.make_async_remote_copy(
            src_ref=region, dst_ref=region, send_sem=send_sem.at[index], recv_sem=recv_sem.at[index],
            device_id=device(flip=1), device_id_type=MESH,
        ).wait_send()

    def y_rows(k):
        return pl.ds(pl.multiple_of(DIRECT + SLICE * ((y + k + 4) % 4), 16), SLICE)

    def kind_rows(kind):
        return y_rows(0) if kind == 0 else pl.ds(0, DIRECT)

    def w_at(r, j, rows):
        if r == 3:
            return weights.at[3, rows, pl.ds(PIECE * j, PIECE)]
        return weights.at[1 + j, rows, pl.ds(PIECE * (r - 1), PIECE)]

    def s_at(r, q):
        if r == 0:
            return states.at[0, 0, pl.ds(128 * q, 128)]
        return states.at[1 + q // 2, 0, pl.ds(256 * (r - 1) + 128 * (q % 2), 128)]

    def x_own(kind, j, side):
        return kind * 4 + j * 2 + side

    def x_fwd(kind, j):
        return 8 + kind * 2 + j

    def y_own(r, j, side):
        return 12 + (r - 1) * 4 + j * 2 + side

    def y_fwd(r, j):
        return 24 + (r - 1) * 2 + j

    def z_own(q, side):
        return 30 + q * 2 + side

    def z_fwd(h):
        return 38 + h

    def pair(s):
        return 40 + s

    def swap(r, flip):
        return 44 + r * 2 + flip

    wide_first = pl.multiple_of(c * (1920 - WIDE), LANES)
    load_h = pltpu.make_async_copy(hidden_ref, hid, local_sem.at[0])
    load_d = pltpu.make_async_copy(dense_ref, den, local_sem.at[1])
    load_w = pltpu.make_async_copy(weight_ref.at[:, pl.ds(wide_first, WIDE)], weights.at[0], local_sem.at[2])
    load_d.start()
    load_h.start()
    load_w.start()
    barrier = pltpu.get_barrier_semaphore()
    friends = [(dx, 0, 0, f) for dx in range(4) for f in range(2) if (dx, f) != (0, 0)]
    friends += [(0, 1, 0, 0), (0, -1, 0, 0), (0, 0, 1, 0), (0, 0, -1, 0)]
    for dx, dy, dz, f in friends:
        pl.semaphore_signal(barrier, inc=1, device_id=device(dx, dy, dz, f), device_id_type=MESH)
    pl.semaphore_wait(barrier, len(friends))

    def send_own_w(kind, j):
        for side, dx in ((0, 1), (1, -1)):
            send(
                x_own(kind, j, side),
                weight_ref.at[kind_rows(kind), pl.ds(pl.multiple_of(wide_first + PIECE * j, LANES), PIECE)],
                w_at(1 + side, j, kind_rows(kind)),
                device(dx=dx),
            )

    def fwd_w(kind, j):
        source = weights.at[1 + j, kind_rows(kind), pl.ds(pl.multiple_of(PIECE * c, LANES), PIECE)]
        send(x_fwd(kind, j), source, w_at(3, j, kind_rows(kind)), device(dx=sign))

    def got_own_w(kind, j):
        for side in range(2):
            got(x_own(kind, j, side), w_at(1 + side, j, kind_rows(kind)))

    def share_w(r, j):
        for side, dy in ((0, 1), (1, -1)):
            send(y_own(r, j, side), w_at(r, j, y_rows(0)), w_at(r, j, y_rows(0)), device(dy=dy))

    def relay_w(r, j):
        got(y_own(r, j, 0), w_at(r, j, y_rows(-1)))
        got(y_own(r, j, 1), w_at(r, j, y_rows(1)))
        send(y_fwd(r, j), w_at(r, j, y_rows(-sign)), w_at(r, j, y_rows(-sign)), device(dy=sign))

    def relayed_w(r, j):
        got(y_fwd(r, j), w_at(r, j, y_rows(2)))

    def send_own_s(q):
        for side, dz in ((0, 1), (1, -1)):
            send(z_own(q, side), s_at(0, q), s_at(1 + side, q), device(dz=dz))

    def relay_s(h):
        for q in (2 * h, 2 * h + 1):
            for side in range(2):
                got(z_own(q, side), s_at(1 + side, q))
        source = states.at[1 + h, 0, pl.ds(pl.multiple_of(256 * c, 256), 256)]
        send(z_fwd(h), source, states.at[3, 0, pl.ds(256 * h, 256)], device(dz=sign))

    def pair_s(s):
        send(pair(s), states.at[s, 0], states.at[s, 1], device(flip=1))

    def paired_s(s):
        got(pair(s), states.at[s, 1])

    send_own_w(0, 0)
    send_own_w(0, 1)
    send_own_w(1, 0)

    load_d.wait()
    load_h.wait()
    gain, shift, offset = gain_ref[...].reshape(1, -1), bias_ref[...].reshape(1, -1), b_ref[...].reshape(1, -1)

    def head(q, first):
        pre = jnp.dot(hid[128 * q:128 * q + 128, :], den[...], preferred_element_type=jnp.float32) + offset
        act = 0.5 * pre * (1.0 + lax.erf(pre * (0.5 ** 0.5)))
        centered = act - jnp.mean(act, axis=-1, keepdims=True)
        spread = jnp.mean(centered * centered, axis=-1, keepdims=True)
        normed = centered * lax.rsqrt(spread + 1e-06) * gain + shift
        if q % 2 == 0:
            first = normed[0:1, :]
        places = 128 * (q % 2) + lax.broadcasted_iota(jnp.int32, normed.shape, 0)
        normed = jnp.where(places < lengths_ref[2 * v + q // 2], normed, first)
        states[0, 0, 128 * q:128 * q + 128, :] = normed.astype(jnp.bfloat16)
        return first

    first = head(0, None)
    for q in range(1, 4):
        first = head(q, first)
        send_own_s(q - 1)
    load_w.wait()

    def event_0():
        got_own_w(0, 0)
        share_w(1, 0)
        share_w(2, 0)
        fwd_w(0, 0)
        send_own_s(3)
        pair_s(0)
        paired_s(0)

    def event_1():
        got_own_w(0, 1)
        share_w(1, 1)
        share_w(2, 1)
        fwd_w(0, 1)
        send_own_w(1, 1)
        relay_w(1, 0)
        relay_w(2, 0)
        relay_s(0)
        pair_s(1)
        paired_s(1)

    def event_2():
        got_own_w(1, 0)
        fwd_w(1, 0)
        relayed_w(1, 0)
        relayed_w(2, 0)

    def event_3():
        relay_w(1, 1)
        relay_w(2, 1)
        for j in range(2):
            got(x_fwd(0, j), w_at(3, j, kind_rows(0)))
            share_w(3, j)

    def event_4():
        relay_s(1)
        pair_s(2)
        paired_s(2)

    def event_6():
        relayed_w(1, 1)
        relayed_w(2, 1)
        got_own_w(1, 1)
        fwd_w(1, 1)

    def event_7():
        relay_w(3, 0)
        relay_w(3, 1)

    def event_9():
        for h in range(2):
            got(z_fwd(h), states.at[3, 0, pl.ds(256 * h, 256)])
        pair_s(3)
        paired_s(3)

    def event_12():
        for j in range(2):
            got(x_fwd(1, j), w_at(3, j, kind_rows(1)))
            relayed_w(3, j)

    events = {0: event_0, 1: event_1, 2: event_2, 3: event_3, 4: event_4, 6: event_6, 7: event_7, 9: event_9, 12: event_12}

    def step(n, _):
        for k, event in events.items():
            pl.when(n == k)(event)
        s = sum(jnp.where(n == k, sk, 0) for k, (sk, _) in enumerate(ORDER) if sk)
        w = sum(jnp.where(n == k, wk, 0) for k, (_, wk) in enumerate(ORDER) if wk)
        for cc in range(2):
            for piece in range(2):
                for hh in range(2):
                    d = jnp.dot(
                        states[s, cc, 256 * hh:256 * hh + 256, :],
                        weights[w, :, PIECE * piece:PIECE * piece + PIECE],
                        preferred_element_type=jnp.float32,
                    )
                    tops[w, s, cc, hh, :, PIECE * piece:PIECE * piece + PIECE] = jnp.max(d.reshape(32, 8, PIECE), axis=0)
        return 0

    lax.fori_loop(0, len(ORDER), step, 0)

    for s in range(4):
        for hh in range(2):
            r, h = ((0, hh), (1 + hh, 0), (1 + hh, 1), (3, hh))[s]
            row = 2 * ((z + DELTA[r] + 4) % 4) + h
            for cc in range(2):
                for w in range(4):
                    best = jnp.max(tops[w, s, cc, hh], axis=0, keepdims=True)
                    for piece in range(2):
                        slot, col = ((0, piece), (1 + piece, 0), (1 + piece, 1), (3, piece))[w]
                        pooled[slot, cc, pl.ds(row, 1), PIECE * col:PIECE * col + PIECE] = best[:, PIECE * piece:PIECE * piece + PIECE]
    back = (0, 2, 1, 3)
    for slot in (3, 1, 2, 0):
        for cc in range(2):
            if (slot, cc) != (0, 0):
                send(swap(slot, cc), pooled.at[slot, cc], landed.at[cc, back[slot]], device(dx=DELTA[slot], flip=cc))
    landed[0, 0] = pooled[0, 0]
    for slot in range(4):
        for cc in range(2):
            if (slot, cc) != (0, 0):
                got(swap(slot, cc), landed.at[cc, back[slot]])
    bias = vbias_ref[...].astype(jnp.float32)
    columns = 1920 * v + lax.broadcasted_iota(jnp.int32, (8, 1920), 1)
    for slot in range(4):
        raw = jnp.concatenate([landed[c, slot], landed[1 - c, slot][:, 2 * WIDE - 1920:]], axis=1) + bias
        done = jnp.where(columns < VOCAB, jnp.log1p(jnp.maximum(raw, 0.0)), 0.0)
        out_ref[pl.ds(pl.multiple_of(8 * ((x + DELTA[slot] + 4) % 4), 8), 8), :] = done

    for kind in range(2):
        for j in range(2):
            for side in range(2):
                left(x_own(kind, j, side), w_at(1 + side, j, kind_rows(kind)))
            left(x_fwd(kind, j), w_at(3, j, kind_rows(kind)))
    for r in range(1, 4):
        for j in range(2):
            for side in range(2):
                left(y_own(r, j, side), w_at(r, j, y_rows(0)))
            left(y_fwd(r, j), w_at(r, j, y_rows(0)))
    for q in range(4):
        for side in range(2):
            left(z_own(q, side), s_at(0, q))
    for h in range(2):
        left(z_fwd(h), states.at[3, 0, pl.ds(256 * h, 256)])
    for s in range(4):
        left(pair(s), states.at[s, 0])
    for slot in range(4):
        for cc in range(2):
            if (slot, cc) != (0, 0):
                left(swap(slot, cc), pooled.at[slot, cc])


MESSAGES = 52


def encode(hidden, dense_w, dense_b, norm_gain, norm_bias, vocabulary_weight, vocabulary_bias, lengths):
    anywhere = pl.BlockSpec(memory_space=pl.ANY)
    vmem = pl.BlockSpec(memory_space=pltpu.VMEM)
    return pl.pallas_call(
        encode_kernel,
        in_specs=[pl.BlockSpec(memory_space=pltpu.SMEM), anywhere, anywhere, vmem, vmem, vmem, anywhere, vmem],
        out_specs=vmem,
        out_shape=jax.ShapeDtypeStruct((32, 1920), jnp.float32),
        scratch_shapes=[
            pltpu.VMEM((512, 768), jnp.bfloat16),
            pltpu.VMEM((768, 768), jnp.bfloat16),
            pltpu.VMEM((4, 2, 512, 768), jnp.bfloat16),
            pltpu.VMEM((4, 768, WIDE), jnp.bfloat16),
            pltpu.VMEM((4, 4, 2, 2, 8, WIDE), jnp.float32),
            pltpu.VMEM((4, 2, 8, WIDE), jnp.float32),
            pltpu.VMEM((2, 4, 8, WIDE), jnp.float32),
            pltpu.SemaphoreType.DMA((3,)),
            pltpu.SemaphoreType.DMA((MESSAGES,)),
            pltpu.SemaphoreType.DMA((MESSAGES,)),
        ],
        compiler_params=pltpu.CompilerParams(collective_id=0, has_side_effects=True, vmem_limit_bytes=56 * 2**20),
    )(lengths, hidden, dense_w, dense_b, norm_gain, norm_bias, vocabulary_weight, vocabulary_bias[None])


def pick_kernel(where_ref, terms_ref, vectors_ref, out_ref, codes):
    passages, places = terms_ref.shape
    first, first_passage = where_ref[0], where_ref[1]
    groups = vectors_ref.shape[1] // LANES
    out_ref[...] = jnp.zeros_like(out_ref)
    k_row = (lax.broadcasted_iota(jnp.int32, (1, places), 1) + 1).astype(jnp.float32)
    j_col = lax.broadcasted_iota(jnp.int32, (16, places), 0)
    o_col = lax.broadcasted_iota(jnp.int32, (LANES, places), 0)
    for p in range(passages):
        t = terms_ref[p:p + 1, :]
        rel = t - first
        j = jnp.where((t >= 0) & (rel >= 0), rel // LANES, 99)
        a = jnp.where(j_col == j, k_row, 0.0).astype(jnp.bfloat16)
        b = jnp.where(o_col == t % LANES, 1.0, 0.0).astype(jnp.bfloat16)
        found = lax.dot_general(a, b, (((1,), (1,)), ((), ())), preferred_element_type=jnp.float32)
        found = found.astype(jnp.int32)
        codes[:, p, :] = jnp.where(found > 0, p * places + found - 1, BIG)
    last = jnp.full((1, LANES), -1, jnp.int32)
    lane = lax.broadcasted_iota(jnp.int32, (passages, LANES), 1)
    row = lax.broadcasted_iota(jnp.int32, (passages, LANES), 0)
    for c in range(LIMIT):
        low = jnp.full((passages, LANES), BIG, jnp.int32)
        for j in range(groups):
            code = codes[j]
            low = jnp.minimum(low, jnp.where(code > last, code, BIG))
        low = jnp.min(low, axis=0, keepdims=True)
        weight = jnp.zeros((passages, LANES), jnp.float32)
        key = jnp.zeros((passages, LANES), jnp.int32)
        for j in range(groups):
            hit = (codes[j] == low) & (low < BIG)
            weight = weight + jnp.where(hit, vectors_ref[:, j * LANES:(j + 1) * LANES], 0.0)
            key = key + jnp.where(hit, (first_passage + row) * VOCAB_PADDED + first + j * LANES + lane + 1, 0)
        out_ref[c:c + 1, :] = jnp.sum(weight, axis=0, keepdims=True)
        out_ref[8 + c:9 + c, :] = (jnp.sum(key, axis=0, keepdims=True) - 1).astype(jnp.float32)
        last = low


def pick(term_ids, vectors, first, first_passage):
    where = jnp.stack([first, first_passage]).astype(jnp.int32)
    return pl.pallas_call(
        pick_kernel,
        in_specs=[pl.BlockSpec(memory_space=pltpu.SMEM)] + [pl.BlockSpec(memory_space=pltpu.VMEM)] * 2,
        out_specs=pl.BlockSpec(memory_space=pltpu.VMEM),
        scratch_shapes=[pltpu.VMEM((16,) + term_ids.shape, jnp.int32)],
        out_shape=jax.ShapeDtypeStruct((16, LANES), jnp.float32),
    )(where, term_ids, vectors)


def local(hidden, dense_w, dense_b, norm_gain, norm_bias, vocabulary_weight, vocabulary_bias, lengths, term_ids):
    passages = lengths.shape[0]
    width = vocabulary_weight.shape[1]
    v = lax.axis_index("vocab")
    b = lax.axis_index("batch")
    vectors = encode(hidden, dense_w, dense_b, norm_gain, norm_bias, vocabulary_weight, vocabulary_bias, lengths)
    sent = pick(term_ids, vectors, v * width, b * passages)
    got = lax.all_to_all(sent, ("batch", "vocab"), split_axis=1, concat_axis=1, tiled=True)
    return vectors, got[None, :LIMIT], got[None, 8:8 + LIMIT].astype(jnp.int32)


def solution(mesh):
    in_specs = (
        P(("batch", "vocab"), None), P(), P(), P(), P(),
        P(None, "vocab"), P("vocab"), P("batch"), P("batch", None),
    )
    out_specs = (P("batch", "vocab"), P(("batch", "vocab"), None, None), P(("batch", "vocab"), None, None))
    return jax.shard_map(local, mesh=mesh, in_specs=in_specs, out_specs=out_specs, check_vma=False)
```

time: 175 us -> 90.6 us (0.52)
  waiting for transfers between devices: 92.5 us -> 0 us
  Pallas kernels: 42.5 us -> 67.1 us
  between operations: 14.1 us -> 0.65 us
  local copies, waits for them, and re-layouts: 7.33 us -> 5.04 us
    all_gather x1 -> x0, waiting for transfers between devices: 92.5 us -> none  [local(): gathered = lax.all_gather(states, 'vocab', axis=0, tiled=True)]
    pallas_call x2 -> x1, Pallas kernels: 39.7 us -> 64.2 us  [encode(): pl.pallas_call(encode_kernel, in_specs=[pl.BlockSpec(memory_space=pltpu.S...]
    broadcast_in_dim x4 -> x1, local copies, waits for them, and re-layouts: 3.99 us -> 1.29 us  [encode(): vocabulary_bias[None]]
  transfers between devices with their start and end apart: 1 -> 0, of which waited for: 1 -> 0; matrix products, arithmetic and copies ran while one was open for 0% -> 0% of each run, Pallas kernels for 0% -> 0%
where the time goes in v2:
time: 90.6 us; the launch traced here: 90.3 us
  Pallas kernels  67.1 us (74%)
  blocking collectives  16.7 us (18%)
  local copies, waits for them, and re-layouts  5.04 us (6%)
    pallas_call x1, Pallas kernels, encode(): pl.pallas_call(encode_kernel, in_specs=[pl.BlockSpec(memory_space=pltpu.S...  64.2 us
    all_to_all x1, blocking collectives, local(): lax.all_to_all(sent, ('batch', 'vocab'), split_axis=1, concat_axis=1, til...  16.7 us
    unnamed x3, local copies, waits for them, and re-layouts  2.96 us
    pallas_call x1, Pallas kernels, pick(): pl.pallas_call(pick_kernel, in_specs=[pl.BlockSpec(memory_space=pltpu.SME...  2.89 us

profile of v2, /device:TPU:1, one launch (start us, length us, event | category | flops | bytes accessed | tf_op | source)
XLA Modules:
  0.0 90.3 jit_solution(762086135348901285)
XLA Ops:
  0.6 1.3 %broadcast_in_dim.7.vbias_ref = bf16[1,1920]{1,0:T(2,128)(2,1)} reshape(bf16[1920]{0:T(1024)(128)(2,1)} %param.15) | data formatting | bytes 7680 | tf_op jit(solution)/shard_map/broadcast_in_dim | solution.py:344
  1.9 0.6 pad_add_fusion.where_ref
  2.6 64.2 %shard_map.112.vectors_ref = f32[32,1920]{1,0:T(8,128)} custom-call(s32[32]{0:T(128)} %lengths_ref.1, bf16[512,768]{1,0:T(8,128)(2,1)} %hidden_ref.1, bf16[768,768]{1,0:T(8,128)(2,1)} %dense_ref.1, f32[768]{0:T(1024)} %b_ref.1, f32[768]{0:T(1024)} %gain_ref.1, f32[768]{0:T(1024)} %bias_ref.1, bf16[768,1920]{1,0:T(8,128)(2,1)} %weight_ref.1, ...), custom_call_target="tpu_custom_call" | custom-call | tf_op jit(solution)/shard_map/pallas_call | solution.py:326
  66.8 2.9 %shard_map.113 = f32[16,128]{1,0:T(8,128)} custom-call(s32[2]{0:T(128)} %pad_add_fusion.where_ref, s32[32,128]{1,0:T(8,128)} %terms_ref.1, f32[32,1920]{1,0:T(8,128)} %shard_map.112.vectors_ref), custom_call_target="tpu_custom_call" | custom-call | tf_op jit(solution)/shard_map/pallas_call | solution.py:386
  69.7 0.8 copy.14
  70.4 16.7 %all_to_all.9 = f32[16,128,1]{0,2,1:T(1,128)S(1)} all-to-all(f32[16,128,1]{0,2,1:T(1,128)S(1)} %copy.14), channel_id=1, replica_groups=mesh['batch'=8,'vocab'=16] {'batch','vocab'}, dimensions={1} | all-to-all | bytes 16384 | tf_op jit(solution)/shard_map/all_to_all | solution.py:402
  87.1 0.2 slice_convert_fusion
  87.3 0.7 copy.15
  88.0 0.7 copy.16
  88.6 1.7 %copy.18 = f32[32,1920]{1,0:T(8,128)} copy(f32[32,1920]{1,0:T(8,128)} %shard_map.112.vectors_ref) | data formatting | bytes 491520

commit v3 on v0

v3 whole, which is shorter than its diff:
```python
import jax
import jax.numpy as jnp
from jax import lax
from jax.experimental import pallas as pl
from jax.experimental.pallas import tpu as pltpu
from jax.sharding import PartitionSpec as P

VOCAB = 30522
VOCAB_PADDED = 30720
K = 128
LIMIT = 5
LANES = 128
BIG = 1 << 20
MESH = pl.DeviceIdType.MESH
BLOCK = 1920
WIDE = 1024
PIECE = 512
DIRECT = 320
SLICE = 112
DELTA = (0, -1, 1, 2)

STEPS = (
    ((0, 0), (0, 1), (1, 0), (1, 1)),
    ((2, 0), (2, 1), (0, 2), (1, 2)),
    ((2, 2), (3, 0), (3, 1), (3, 2)),
    ((0, 3), (1, 3), (2, 3), (3, 3)),
    ((4, 0), (4, 1), (4, 2), (4, 3)),
    ((0, 4), (1, 4), (2, 4), (3, 4)),
    ((4, 4), (5, 0), (5, 1), (5, 2)),
    ((5, 3), (5, 4), (0, 5), (1, 5)),
    ((2, 5), (3, 5), (4, 5), (5, 5)),
    ((6, 0), (6, 1), (6, 2), (6, 3)),
    ((6, 4), (6, 5), (0, 6), (1, 6)),
    ((2, 6), (3, 6), (4, 6), (5, 6)),
    ((6, 6), (7, 0), (7, 1), (7, 2)),
    ((7, 3), (7, 4), (7, 5), (7, 6)),
    ((0, 7), (1, 7), (2, 7), (3, 7)),
    ((4, 7), (5, 7), (6, 7), (7, 7)),
)


class Numbers:
    def __init__(self):
        self.known = {}

    def __call__(self, *name):
        return self.known.setdefault(name, len(self.known))


def encode_kernel(
    lengths_ref, hidden_ref, dense_ref, b_ref, gain_ref, bias_ref, weight_ref, vbias_ref, terms_ref,
    out_ref, out_w_ref, out_k_ref,
    hid, den, states, weights, tops, pooled, landed, codes, lows, sheet, boxes, batch_in, vocab_out, vocab_in, sheet_in,
    local_sem, send_sem, recv_sem,
):
    b, v = lax.axis_index("batch"), lax.axis_index("vocab")
    y, c = b // 2, b % 2
    x, z = v // 4, v % 4
    sign = 1 - 2 * c
    number = Numbers()
    started = []

    def device(dx=0, dy=0, dz=0, flip=0):
        core = 1 - c if flip else c
        return (2 * ((y + dy + 4) % 4) + core, 4 * ((x + dx + 4) % 4) + (z + dz + 4) % 4)

    def copy(name, source, target, to):
        i = number(*name)
        return pltpu.make_async_remote_copy(
            src_ref=source, dst_ref=target, send_sem=send_sem.at[i], recv_sem=recv_sem.at[i],
            device_id=to, device_id_type=MESH,
        )

    def send(name, source, target, to):
        copy(name, source, target, to).start()
        started.append(name)

    def got(name, region):
        copy(name, region, region, device(flip=1)).wait_recv()

    def y_rows(k):
        return pl.ds(pl.multiple_of(DIRECT + SLICE * ((y + k + 4) % 4), 16), SLICE)

    def kind_rows(kind):
        return y_rows(0) if kind == 0 else pl.ds(0, DIRECT)

    wide_first = pl.multiple_of(c * (BLOCK - WIDE), LANES)
    load_h = pltpu.make_async_copy(hidden_ref, hid, local_sem.at[0])
    load_d = pltpu.make_async_copy(dense_ref, den, local_sem.at[1])
    load_w = [
        pltpu.make_async_copy(weight_ref.at[:, pl.ds(pl.multiple_of(wide_first + PIECE * i, LANES), PIECE)], weights.at[i], local_sem.at[2 + i])
        for i in range(2)
    ]
    load_d.start()
    load_h.start()
    for load in load_w:
        load.start()
    barrier = pltpu.get_barrier_semaphore()
    friends = [((b + d) % 8, v) for d in range(1, 8)] + [(b, (v + d) % 16) for d in range(1, 16)]
    friends += [device(dx, 0, 0, 1) for dx in range(1, 4)]
    for friend in friends:
        pl.semaphore_signal(barrier, inc=1, device_id=friend, device_id_type=MESH)

    def send_own_w(kind, j):
        for side, dx in ((0, 1), (1, -1)):
            send(
                ("x", kind, j, side),
                weight_ref.at[kind_rows(kind), pl.ds(pl.multiple_of(wide_first + 256 * j, LANES), 256)],
                weights.at[2 + j, kind_rows(kind), pl.ds(256 * side, 256)],
                device(dx=dx),
            )

    def got_own_w(kind, j):
        for side in range(2):
            got(("x", kind, j, side), weights.at[2 + j, kind_rows(kind), pl.ds(256 * side, 256)])

    def fwd_w(kind, i):
        for j in (2 * i, 2 * i + 1):
            source = weights.at[2 + j, kind_rows(kind), pl.ds(pl.multiple_of(256 * c, LANES), 256)]
            send(("xf", kind, j), source, weights.at[6 + i, kind_rows(kind), pl.ds(256 * (j % 2), 256)], device(dx=sign))

    def got_fwd_w(kind, i):
        for j in (2 * i, 2 * i + 1):
            got(("xf", kind, j), weights.at[6 + i, kind_rows(kind), pl.ds(256 * (j % 2), 256)])

    def share_w(m):
        for side, dy in ((0, 1), (1, -1)):
            send(("y", m, side), weights.at[m, y_rows(0)], weights.at[m, y_rows(0)], device(dy=dy))

    def relay_w(m):
        got(("y", m, 0), weights.at[m, y_rows(-1)])
        got(("y", m, 1), weights.at[m, y_rows(1)])
        send(("yf", m), weights.at[m, y_rows(-sign)], weights.at[m, y_rows(-sign)], device(dy=sign))

    def relayed_w(m):
        got(("yf", m), weights.at[m, y_rows(2)])

    def send_own_s(q):
        for side, dz in ((0, 1), (1, -1)):
            send(("z", q, side), states.at[0, pl.ds(128 * q, 128)], states.at[2 + q, pl.ds(128 * side, 128)], device(dz=dz))

    def got_own_s(q):
        for side in range(2):
            got(("z", q, side), states.at[2 + q, pl.ds(128 * side, 128)])

    def fwd_s(h):
        for q in (2 * h, 2 * h + 1):
            source = states.at[2 + q, pl.ds(pl.multiple_of(128 * c, 128), 128)]
            send(("zf", q), source, states.at[6 + h, pl.ds(128 * (q % 2), 128)], device(dz=sign))

    def got_fwd_s(h):
        for q in (2 * h, 2 * h + 1):
            got(("zf", q), states.at[6 + h, pl.ds(128 * (q % 2), 128)])

    def pair_s(k):
        if k == 1:
            send(("d", k), states.at[0], states.at[1], device(flip=1))
        else:
            send(("d", k), states.at[k, pl.ds(0, 256)], states.at[k, pl.ds(256, 256)], device(flip=1))

    def paired_s(k):
        got(("d", k), states.at[1] if k == 1 else states.at[k, pl.ds(256, 256)])

    gain, shift, offset = gain_ref[...].reshape(1, -1), bias_ref[...].reshape(1, -1), b_ref[...].reshape(1, -1)

    def head(q, first):
        pre = jnp.dot(hid[128 * q:128 * q + 128, :], den[...], preferred_element_type=jnp.float32) + offset
        act = 0.5 * pre * (1.0 + lax.erf(pre * (0.5 ** 0.5)))
        centered = act - jnp.mean(act, axis=-1, keepdims=True)
        spread = jnp.mean(centered * centered, axis=-1, keepdims=True)
        normed = centered * lax.rsqrt(spread + 1e-06) * gain + shift
        if q % 2 == 0:
            first = normed[0:1, :]
        places = 128 * (q % 2) + lax.broadcasted_iota(jnp.int32, normed.shape, 0)
        normed = jnp.where(places < lengths_ref[2 * v + q // 2], normed, first)
        states[0, 128 * q:128 * q + 128, :] = normed.astype(jnp.bfloat16)
        return first

    load_d.wait()
    load_h.wait()
    first = head(0, None)
    pl.semaphore_wait(barrier, len(friends))
    for kind, j in ((0, 0), (0, 1), (1, 0), (0, 2), (0, 3), (1, 1)):
        send_own_w(kind, j)
    for q in range(1, 4):
        first = head(q, first)
        send_own_s(q - 1)
    for load in load_w:
        load.wait()

    def find_codes():
        k_row = (lax.broadcasted_iota(jnp.int32, (1, K), 1) + 1).astype(jnp.float32)
        j_col = lax.broadcasted_iota(jnp.int32, (16, K), 0)
        o_col = lax.broadcasted_iota(jnp.int32, (LANES, K), 0)
        start = BLOCK * v
        for p in range(32):
            t = terms_ref[p:p + 1, :]
            rel = t - start
            group = jnp.where((t >= 0) & (rel >= 0), rel // LANES, 99)
            one = jnp.where(j_col == group, k_row, 0.0).astype(jnp.bfloat16)
            two = jnp.where(o_col == t % LANES, 1.0, 0.0).astype(jnp.bfloat16)
            found = lax.dot_general(one, two, (((1,), (1,)), ((), ())), preferred_element_type=jnp.float32).astype(jnp.int32)
            codes[:, p, :] = jnp.where(found > 0, p * K + found - 1, BIG)
        lane = lax.broadcasted_iota(jnp.int32, (32, LANES), 1)
        row = lax.broadcasted_iota(jnp.int32, (32, LANES), 0)
        sheet[...] = jnp.zeros_like(sheet)
        last = jnp.full((1, LANES), -1, jnp.int32)
        for slot in range(LIMIT):
            low = jnp.full((32, LANES), BIG, jnp.int32)
            for j in range(15):
                code = codes[j]
                low = jnp.minimum(low, jnp.where(code > last, code, BIG))
            low = jnp.min(low, axis=0, keepdims=True)
            key = jnp.zeros((32, LANES), jnp.int32)
            for j in range(15):
                hit = (codes[j] == low) & (low < BIG)
                key = key + jnp.where(hit, (32 * b + row) * VOCAB_PADDED + start + j * LANES + lane + 1, 0)
            sheet[8 + slot:9 + slot, :] = (jnp.sum(key, axis=0, keepdims=True) - 1).astype(jnp.float32)
            lows[slot:slot + 1, :] = low
            last = low

    back = (0, 2, 1, 3)

    def pool(slots):
        for r in range(4):
            for h in range(2):
                row = 2 * ((z + DELTA[r] + 4) % 4) + h
                for cc in range(2):
                    if r == 0:
                        parts = ((cc, 2 * h), (cc, 2 * h + 1))
                    elif r == 3:
                        parts = ((6 + h, 2 * cc), (6 + h, 2 * cc + 1))
                    else:
                        parts = ((2 + 2 * h, 2 * cc + r - 1), (3 + 2 * h, 2 * cc + r - 1))
                    for m in range(8):
                        slot = (0, 0, 1, 1, 1, 1, 3, 3)[m]
                        if slot not in slots:
                            continue
                        (k0, g0), (k1, g1) = parts
                        best = jnp.max(jnp.maximum(tops[m, k0, g0], tops[m, k1, g1]), axis=0, keepdims=True)
                        if slot == 1:
                            for i in range(2):
                                pooled[1 + i, cc, pl.ds(row, 1), 256 * (m - 2):256 * (m - 1)] = best[:, 256 * i:256 * i + 256]
                        else:
                            pooled[slot, cc, pl.ds(row, 1), PIECE * (m % 2):PIECE * (m % 2) + PIECE] = best

    def swap(slot):
        for cc in range(2):
            if (slot, cc) != (0, 0):
                send(("e", slot, cc), pooled.at[slot, cc], landed.at[cc, back[slot]], device(dx=DELTA[slot], flip=cc))

    def event_0():
        got_own_w(0, 0)
        share_w(2)
        got_own_w(0, 1)
        share_w(3)
        send_own_s(3)
        pair_s(1)
        fwd_w(0, 0)
        send_own_w(1, 2)
        paired_s(1)

    def event_1():
        got_own_s(0)
        pair_s(2)
        relay_w(2)
        got_own_w(0, 2)
        share_w(4)
        find_codes()
        relay_w(3)
        got_own_w(0, 3)
        share_w(5)
        fwd_w(0, 1)
        send_own_w(1, 3)
        got_own_s(1)
        pair_s(3)
        fwd_s(0)
        paired_s(2)
        got_own_w(1, 0)
        relayed_w(2)

    def event_2():
        paired_s(3)

    def event_3():
        got_own_w(1, 1)
        fwd_w(1, 0)
        relay_w(4)
        relayed_w(3)
        got_own_s(2)
        pair_s(4)

    def event_4():
        got_fwd_w(0, 0)
        share_w(6)
        paired_s(4)

    def event_5():
        relay_w(5)
        relayed_w(4)
        got_own_w(1, 2)

    def event_6():
        got_own_s(3)
        pair_s(5)
        fwd_s(1)
        got_fwd_w(0, 1)
        share_w(7)
        relay_w(6)
        paired_s(5)

    def event_7():
        relayed_w(5)
        got_own_w(1, 3)
        fwd_w(1, 1)

    def event_8():
        relay_w(7)
        got_fwd_s(0)
        pair_s(6)

    def event_9():
        paired_s(6)

    def event_10():
        relayed_w(6)
        got_fwd_w(1, 0)
        got_fwd_s(1)
        pair_s(7)

    def event_12():
        paired_s(7)

    def event_14():
        relayed_w(7)
        got_fwd_w(1, 1)
        pool((0, 1))
        swap(1)
        swap(2)
        swap(0)

    events = (
        event_0, event_1, event_2, event_3, event_4, event_5, event_6, event_7,
        event_8, event_9, event_10, None, event_12, None, event_14, None,
    )

    def step(n, _):
        for at, event in enumerate(events):
            if event is not None:
                pl.when(n == at)(event)
        for part in range(4):
            k = sum(jnp.where(n == at, items[part][0], 0) for at, items in enumerate(STEPS) if items[part][0])
            m = sum(jnp.where(n == at, items[part][1], 0) for at, items in enumerate(STEPS) if items[part][1])
            d = jnp.dot(states[k], weights[m], preferred_element_type=jnp.float32)
            tops[m, k] = jnp.max(d.reshape(4, 16, 8, PIECE), axis=1)
        return 0

    lax.fori_loop(0, len(STEPS), step, 0)
    pool((3,))
    swap(3)
    landed[0, 0] = pooled[0, 0]
    bias = vbias_ref[...].astype(jnp.float32)
    columns = BLOCK * v + lax.broadcasted_iota(jnp.int32, (8, BLOCK), 1)
    for slot in (0, 1, 2, 3):
        for cc in range(2):
            if (slot, cc) != (0, 0):
                got(("e", back[slot], cc), landed.at[cc, slot])
        raw = jnp.concatenate([landed[c, slot], landed[1 - c, slot][:, 2 * WIDE - BLOCK:]], axis=1) + bias
        done = jnp.where(columns < VOCAB, jnp.log1p(jnp.maximum(raw, 0.0)), 0.0)
        out_ref[pl.ds(pl.multiple_of(8 * ((x + DELTA[slot] + 4) % 4), 8), 8), :] = done

    for slot in range(LIMIT):
        low = lows[slot:slot + 1, :]
        weight = jnp.zeros((32, LANES), jnp.float32)
        for j in range(15):
            hit = (codes[j] == low) & (low < BIG)
            weight = weight + jnp.where(hit, out_ref[:, j * LANES:(j + 1) * LANES], 0.0)
        sheet[slot:slot + 1, :] = jnp.sum(weight, axis=0, keepdims=True)
    boxes[...] = jnp.transpose(sheet[...]).reshape(8, 16, LANES)
    for d in range(1, 8):
        to = (b + d) % 8
        send(("pb", d), boxes.at[to], batch_in.at[b], (to, v))
    batch_in[b] = boxes[b]
    for d in range(1, 8):
        got(("pb", d), batch_in.at[(b - d + 8) % 8])
    for origin in range(8):
        vocab_out[:, origin, :] = batch_in[origin]
    for d in range(1, 16):
        to = (v + d) % 16
        send(("pv", d), vocab_out.at[to], vocab_in.at[v], (b, to))
    vocab_in[v] = vocab_out[v]
    for d in range(1, 16):
        got(("pv", d), vocab_in.at[(v - d + 16) % 16])
    for origin in range(16):
        sheet_in[:, origin, :] = vocab_in[origin]
    result = jnp.transpose(sheet_in[...].reshape(LANES, LANES))
    out_w_ref[...] = result[0:LIMIT]
    out_k_ref[...] = result[8:8 + LIMIT].astype(jnp.int32)

    def shape_of(name):
        if name[0] in ("x", "xf"):
            return weights.at[2, pl.ds(0, DIRECT if name[1] else SLICE), pl.ds(0, 256)]
        return {
            "y": weights.at[2, pl.ds(0, SLICE)],
            "yf": weights.at[2, pl.ds(0, SLICE)],
            "z": states.at[0, pl.ds(0, 128)],
            "zf": states.at[0, pl.ds(0, 128)],
            "d": states.at[0] if name[1] == 1 else states.at[0, pl.ds(0, 256)],
            "e": pooled.at[0, 0],
            "pb": boxes.at[0],
            "pv": vocab_out.at[0],
        }[name[0]]

    for name in started:
        copy(name, shape_of(name), shape_of(name), device(flip=1)).wait_send()


MESSAGES = 96


def encode(hidden, dense_w, dense_b, norm_gain, norm_bias, vocabulary_weight, vocabulary_bias, lengths, term_ids):
    anywhere = pl.BlockSpec(memory_space=pl.ANY)
    vmem = pl.BlockSpec(memory_space=pltpu.VMEM)
    smem = pl.BlockSpec(memory_space=pltpu.SMEM)
    return pl.pallas_call(
        encode_kernel,
        in_specs=[smem, anywhere, anywhere, vmem, vmem, vmem, anywhere, vmem, vmem],
        out_specs=[vmem, vmem, vmem],
        out_shape=[
            jax.ShapeDtypeStruct((32, BLOCK), jnp.float32),
            jax.ShapeDtypeStruct((LIMIT, LANES), jnp.float32),
            jax.ShapeDtypeStruct((LIMIT, LANES), jnp.int32),
        ],
        scratch_shapes=[
            pltpu.VMEM((512, 768), jnp.bfloat16),
            pltpu.VMEM((768, 768), jnp.bfloat16),
            pltpu.VMEM((8, 512, 768), jnp.bfloat16),
            pltpu.VMEM((8, 768, PIECE), jnp.bfloat16),
            pltpu.VMEM((8, 8, 4, 8, PIECE), jnp.float32),
            pltpu.VMEM((4, 2, 8, WIDE), jnp.float32),
            pltpu.VMEM((2, 4, 8, WIDE), jnp.float32),
            pltpu.VMEM((16, 32, LANES), jnp.int32),
            pltpu.VMEM((8, LANES), jnp.int32),
            pltpu.VMEM((LANES, LANES), jnp.float32),
            pltpu.VMEM((8, 16, LANES), jnp.float32),
            pltpu.VMEM((8, 16, LANES), jnp.float32),
            pltpu.VMEM((16, 8, LANES), jnp.float32),
            pltpu.VMEM((16, 8, LANES), jnp.float32),
            pltpu.VMEM((8, 16, LANES), jnp.float32),
            pltpu.SemaphoreType.DMA((4,)),
            pltpu.SemaphoreType.DMA((MESSAGES,)),
            pltpu.SemaphoreType.DMA((MESSAGES,)),
        ],
        compiler_params=pltpu.CompilerParams(collective_id=0, has_side_effects=True, vmem_limit_bytes=56 * 2**20),
    )(lengths, hidden, dense_w, dense_b, norm_gain, norm_bias, vocabulary_weight, vocabulary_bias, term_ids)


def local(hidden, dense_w, dense_b, norm_gain, norm_bias, vocabulary_weight, vocabulary_bias, lengths, term_ids):
    vectors, weights, keys = encode(
        hidden, dense_w, dense_b, norm_gain, norm_bias, vocabulary_weight, vocabulary_bias[None], lengths, term_ids
    )
    return vectors, weights[None], keys[None]


def solution(mesh):
    in_specs = (
        P(("batch", "vocab"), None), P(), P(), P(), P(),
        P(None, "vocab"), P("vocab"), P("batch"), P("batch", None),
    )
    out_specs = (P("batch", "vocab"), P(("batch", "vocab"), None, None), P(("batch", "vocab"), None, None))
    return jax.shard_map(local, mesh=mesh, in_specs=in_specs, out_specs=out_specs, check_vma=False)
```

time: 265 us -> 76.9 us (0.29)
  matrix products: 84.2 us -> 0 us
  Pallas kernels: 0 us -> 70.5 us
  waiting for transfers between devices: 69.7 us -> 0 us
  local copies, waits for them, and re-layouts: 70.2 us -> 5.46 us
  starting transfers between devices: 19.6 us -> 0 us
  between operations: 14.3 us -> 0.64 us
  other arithmetic: 5.67 us -> 0 us
    dot_general x17 -> x0, matrix products: 84.2 us -> none  [the longest x16 79 us: pool_block(): jnp.dot(normed, columns_w, preferred_element_type=jnp.float32) + bias_wide]
    pallas_call x0 -> x1, Pallas kernels: none -> 70.5 us  [encode(): pl.pallas_call(encode_kernel, in_specs=[smem, anywhere, anywhere, vmem, v...]
    all_gather x1 -> x0, waiting for transfers between devices: 60.8 us -> none  [local(): gathered = lax.all_gather(source_rows, 'vocab', axis=0, tiled=True)]
    gather x1 -> x0, local copies, waits for them, and re-layouts: 32.8 us -> none  [local(): picked = vectors[row_index, local_columns]]
    unnamed x20 -> x3, local copies, waits for them, and re-layouts: 32.6 us -> 4.17 us
    all_to_all x2 -> x0, starting transfers between devices: 19.5 us -> none  [the longest x1 11.5 us: local(): lax.all_to_all(send_keys, ('batch', 'vocab'), split_axis=1, concat_axis=1...]
    all_to_all x2 -> x0, waiting for transfers between devices: 8.91 us -> none  [the longest x1 8.9 us: local(): lax.all_to_all(send_weights, ('batch', 'vocab'), split_axis=1, concat_axi...]
    all_to_all x4 -> x0, local copies, waits for them, and re-layouts: 2.76 us -> none  [the longest x2 1.38 us: local(): lax.all_to_all(send_weights, ('batch', 'vocab'), split_axis=1, concat_axi...]
  transfers between devices with their start and end apart: 3 -> 0, of which waited for: 2 -> 0; matrix products, arithmetic and copies ran while one was open for 57% -> 0% of each run, Pallas kernels for 0% -> 0%
where the time goes in v3:
time: 76.9 us; the launch traced here: 76.6 us
  Pallas kernels  70.5 us (92%)
  local copies, waits for them, and re-layouts  5.46 us (7%)
    pallas_call x1, Pallas kernels, encode(): pl.pallas_call(encode_kernel, in_specs=[smem, anywhere, anywhere, vmem, v...  70.5 us
    unnamed x3, local copies, waits for them, and re-layouts  4.17 us

profile of v3, /device:TPU:1, one launch (start us, length us, event | category | flops | bytes accessed | tf_op | source)
XLA Modules:
  0.0 76.6 jit_solution(6036361637553438595)
XLA Ops:
  0.6 1.3 %broadcast_in_dim.9.vbias_ref = bf16[1,1920]{1,0:T(2,128)(2,1)} reshape(bf16[1920]{0:T(1024)(128)(2,1)} %param.15) | data formatting | bytes 7680 | tf_op jit(solution)/shard_map/broadcast_in_dim | solution.py:460
  1.9 70.5 %shard_map.112 = (f32[32,1920]{1,0:T(8,128)}, f32[5,128]{1,0:T(8,128)}, s32[5,128]{1,0:T(8,128)}) custom-call(s32[32]{0:T(128)} %lengths_ref.1, bf16[512,768]{1,0:T(8,128)(2,1)} %hidden_ref.1, bf16[768,768]{1,0:T(8,128)(2,1)} %dense_ref.1, f32[768]{0:T(1024)} %b_ref.1, f32[768]{0:T(1024)} %gain_ref.1, f32[768]{0:T(1024)} %bias_ref.1, ...), custom_call_target="tpu_custom_call" | custom-call | tf_op jit(solution)/shard_map/pallas_call | solution.py:425
  72.4 1.3 %copy.12 = f32[1,5,128]{2,0,1:T(1,128)} copy(f32[1,5,128]{2,1,0:T(8,128)} %bitcast.3) | data formatting | bytes 5120
  73.7 1.3 %copy.13 = s32[1,5,128]{2,0,1:T(1,128)} copy(s32[1,5,128]{2,1,0:T(8,128)} %bitcast.2) | data formatting | bytes 5120
  75.0 1.7 %copy.15 = f32[32,1920]{1,0:T(8,128)} copy(f32[32,1920]{1,0:T(8,128)} %get-tuple-element.15) | data formatting | bytes 491520

commit v4 on v3

v4 whole, which is shorter than its diff:
```python
import jax
import jax.numpy as jnp
from jax import lax
from jax.experimental import pallas as pl
from jax.experimental.pallas import tpu as pltpu
from jax.sharding import PartitionSpec as P

VOCAB = 30522
VOCAB_PADDED = 30720
K = 128
LIMIT = 5
LANES = 128
BIG = 1 << 20
MESH = pl.DeviceIdType.MESH
BLOCK = 1920
WIDE = 1024
PIECE = 512
DIRECT = (640, 256, 256, 256)
SLICE = tuple((768 - rows) // 4 for rows in DIRECT)
DELTA = (0, -1, 1, 2)

FIRST = (
    ((("own_s", 3), ("pair", 1)), ((0, 0), (0, 1))),
    ((("share", 2), ("share", 3), ("rows", 1)), ((1, 0), (1, 1))),
)
FOURS = (
    (
        (("across", 0, 0), ("own_w", 1, 2), ("codes",), ("relay", 2), ("pair", 2), ("rows", 2), ("relay", 3), ("columns", 2)),
        ((0, 2), (1, 2), (2, 0), (2, 1)),
    ),
    ((("share", 4), ("pair", 3), ("far", 0), ("rows", 3)), ((2, 2), (3, 0), (3, 1), (3, 2))),
    (
        (("share", 5), ("across", 0, 1), ("own_w", 1, 3), ("pair", 4), ("columns", 3)),
        ((0, 3), (1, 3), (2, 3), (3, 3)),
    ),
    ((("across", 1, 0), ("relay", 4), ("rows", 4)), ((4, 0), (4, 1), (4, 2), (4, 3))),
    ((("pair", 5), ("far", 1), ("relay", 5), ("share", 6), ("columns", 4)), ((0, 4), (1, 4), (2, 4), (3, 4))),
    ((("share", 7), ("across", 1, 1), ("rows", 5)), ((4, 4), (5, 0), (5, 1), (5, 2))),
)
EIGHTS = (
    (
        (("relay", 6), ("columns", 5), ("pair", 6)),
        ((5, 3), (5, 4), (0, 5), (1, 5), (2, 5), (3, 5), (4, 5), (5, 5)),
    ),
    (
        (("relay", 7), ("rows", 6), ("columns", 6), ("pair", 7)),
        ((6, 0), (6, 1), (6, 2), (6, 3), (6, 4), (6, 5), (0, 6), (1, 6)),
    ),
    ((("rows", 7),), ((2, 6), (3, 6), (4, 6), (5, 6), (6, 6), (7, 0), (7, 1), (7, 2))),
    ((("columns", 7),), ((7, 3), (7, 4), (7, 5), (7, 6), (0, 7), (1, 7), (2, 7), (3, 7))),
)
LAST = (((("early",),), ((4, 7), (5, 7), (6, 7), (7, 7))),)


class Numbers:
    def __init__(self):
        self.known = {}

    def __call__(self, *name):
        return self.known.setdefault(name, len(self.known))


def encode_kernel(
    lengths_ref, hidden_ref, dense_ref, b_ref, gain_ref, bias_ref, weight_ref, vbias_ref, terms_ref,
    out_ref, sheet_out_ref,
    hid, den, states, weights, tops, pooled, landed, codes, lows, sheet, boxes, batch_in, vocab_out, vec,
    local_sem, send_sem, recv_sem,
):
    b, v = lax.axis_index("batch"), lax.axis_index("vocab")
    y, c = b // 2, b % 2
    x, z = v // 4, v % 4
    sign = 1 - 2 * c
    number = Numbers()
    started = []

    def device(dx=0, dy=0, dz=0, flip=0):
        core = 1 - c if flip else c
        return (2 * ((y + dy + 4) % 4) + core, 4 * ((x + dx + 4) % 4) + (z + dz + 4) % 4)

    def copy(name, source, target, to):
        i = number(*name)
        assert i < MESSAGES
        return pltpu.make_async_remote_copy(
            src_ref=source, dst_ref=target, send_sem=send_sem.at[i], recv_sem=recv_sem.at[i],
            device_id=to, device_id_type=MESH,
        )

    def send(name, source, target, to):
        copy(name, source, target, to).start()
        if name not in started:
            started.append(name)

    waited = []

    def once(name, act):
        if name not in waited:
            waited.append(name)
            act()

    def got(name, region):
        copy(name, region, region, device(flip=1)).wait_recv()

    def y_rows(j, k):
        return pl.ds(pl.multiple_of(DIRECT[j] + SLICE[j] * ((y + k + 4) % 4), 16), SLICE[j])

    def kind_rows(kind, j):
        return y_rows(j, 0) if kind == 0 else pl.ds(0, DIRECT[j])

    def by_core(j, act):
        if j:
            act(0, 256)
        else:
            pl.when(c == 0)(lambda: act(0, 256))
            pl.when(c == 1)(lambda: act(128, 128))

    wide_first = pl.multiple_of(c * (BLOCK - WIDE), LANES)
    load_h = pltpu.make_async_copy(hidden_ref, hid, local_sem.at[0])
    load_d = pltpu.make_async_copy(dense_ref, den, local_sem.at[1])
    load_w = [
        pltpu.make_async_copy(weight_ref.at[:, pl.ds(pl.multiple_of(wide_first + PIECE * i, LANES), PIECE)], weights.at[i], local_sem.at[2 + i])
        for i in range(2)
    ]
    load_d.start()
    load_h.start()
    for load in load_w:
        load.start()
    barrier = pltpu.get_barrier_semaphore()
    friends = [((b + d) % 8, v) for d in range(1, 8)] + [(b, (v + d) % 16) for d in range(1, 16)]
    friends += [device(dx, 0, 0, 1) for dx in range(1, 4)]
    for friend in friends:
        pl.semaphore_signal(barrier, inc=1, device_id=friend, device_id_type=MESH)

    def send_own_w(kind, j):
        def act(first, width):
            for side, dx in ((0, 1), (1, -1)):
                send(
                    ("x", kind, j, side),
                    weights.at[j // 2, kind_rows(kind, j), pl.ds(256 * (j % 2) + first, width)],
                    weights.at[2 + j, kind_rows(kind, j), pl.ds(256 * side + first, width)],
                    device(dx=dx),
                )

        by_core(j, act)

    def got_own_w(kind, j):
        def act(first, width):
            for side in range(2):
                got(("x", kind, j, side), weights.at[2 + j, kind_rows(kind, j), pl.ds(256 * side + first, width)])

        once(("x", kind, j), lambda: by_core(j, act))

    def fwd_w(kind, i):
        for j in (2 * i, 2 * i + 1):
            got_own_w(kind, j)

            def act(first, width):
                source = weights.at[2 + j, kind_rows(kind, j), pl.ds(pl.multiple_of(256 * c + first, LANES), width)]
                target = weights.at[6 + i, kind_rows(kind, j), pl.ds(256 * (j % 2) + first, width)]
                send(("xf", kind, j), source, target, device(dx=sign))

            by_core(j, act)

    def got_fwd_w(kind, i):
        for j in (2 * i, 2 * i + 1):
            by_core(j, lambda first, width: got(("xf", kind, j), weights.at[6 + i, kind_rows(kind, j), pl.ds(256 * (j % 2) + first, width)]))

    def strips(m):
        return ((m - 2, 0), (m - 2, 256)) if m < 6 else ((2 * m - 12, 0), (2 * m - 11, 256))

    def share_w(m):
        got_own_w(0, m - 2) if m < 6 else got_fwd_w(0, m - 6)
        for j, at in strips(m):
            def act(first, width):
                piece = weights.at[m, y_rows(j, 0), pl.ds(at + first, width)]
                for side, dy in ((0, 1), (1, -1)):
                    send(("y", m, at, side), piece, piece, device(dy=dy))

            by_core(j, act)

    def relay_w(m):
        for j, at in strips(m):
            def act(first, width):
                got(("y", m, at, 0), weights.at[m, y_rows(j, -1), pl.ds(at + first, width)])
                got(("y", m, at, 1), weights.at[m, y_rows(j, 1), pl.ds(at + first, width)])
                piece = weights.at[m, y_rows(j, -sign), pl.ds(at + first, width)]
                send(("yf", m, at), piece, piece, device(dy=sign))

            by_core(j, act)

    def ready_w(m):
        for j, at in strips(m):
            by_core(j, lambda first, width: got(("yf", m, at), weights.at[m, y_rows(j, 2), pl.ds(at + first, width)]))
        got_own_w(1, m - 2) if m < 6 else got_fwd_w(1, m - 6)

    def send_own_s(q):
        for side, dz in ((0, 1), (1, -1)):
            send(("z", q, side), states.at[0, pl.ds(128 * q, 128)], states.at[2 + q, pl.ds(128 * side, 128)], device(dz=dz))

    def got_own_s(q):
        def act():
            for side in range(2):
                got(("z", q, side), states.at[2 + q, pl.ds(128 * side, 128)])

        once(("z", q), act)

    def fwd_s(h):
        for q in (2 * h, 2 * h + 1):
            got_own_s(q)
            source = states.at[2 + q, pl.ds(pl.multiple_of(128 * c, 128), 128)]
            send(("zf", q), source, states.at[6 + h, pl.ds(128 * (q % 2), 128)], device(dz=sign))

    def got_fwd_s(h):
        for q in (2 * h, 2 * h + 1):
            got(("zf", q), states.at[6 + h, pl.ds(128 * (q % 2), 128)])

    def pair_s(k):
        if k >= 6:
            got_fwd_s(k - 6)
        elif k >= 2:
            got_own_s(k - 2)
        if k == 1:
            send(("d", k), states.at[0], states.at[1], device(flip=1))
        else:
            send(("d", k), states.at[k, pl.ds(0, 256)], states.at[k, pl.ds(256, 256)], device(flip=1))

    def paired_s(k):
        got(("d", k), states.at[1] if k == 1 else states.at[k, pl.ds(256, 256)])

    gain, shift, offset = gain_ref[...].reshape(1, -1), bias_ref[...].reshape(1, -1), b_ref[...].reshape(1, -1)

    def head(q, first):
        pre = jnp.dot(hid[128 * q:128 * q + 128, :], den[...], preferred_element_type=jnp.float32) + offset
        act = 0.5 * pre * (1.0 + lax.erf(pre * (0.5 ** 0.5)))
        centered = act - jnp.mean(act, axis=-1, keepdims=True)
        spread = jnp.mean(centered * centered, axis=-1, keepdims=True)
        normed = centered * lax.rsqrt(spread + 1e-06) * gain + shift
        if q % 2 == 0:
            first = normed[0:1, :]
        places = 128 * (q % 2) + lax.broadcasted_iota(jnp.int32, normed.shape, 0)
        normed = jnp.where(places < lengths_ref[2 * v + q // 2], normed, first)
        states[0, 128 * q:128 * q + 128, :] = normed.astype(jnp.bfloat16)
        return first

    load_d.wait()
    load_h.wait()
    first = head(0, None)
    for load in load_w:
        load.wait()
    pl.semaphore_wait(barrier, len(friends))
    for kind, j in ((0, 0), (0, 1), (1, 0), (0, 2), (0, 3), (1, 1)):
        send_own_w(kind, j)
    send_own_s(0)
    for q in range(1, 4):
        first = head(q, first)
        if q > 1:
            send_own_s(q - 1)

    def find_codes():
        k_row = (lax.broadcasted_iota(jnp.int32, (1, K), 1) + 1).astype(jnp.float32)
        j_col = lax.broadcasted_iota(jnp.int32, (16, K), 0)
        o_col = lax.broadcasted_iota(jnp.int32, (LANES, K), 0)
        start = BLOCK * v
        for p in range(32):
            t = terms_ref[p:p + 1, :]
            rel = t - start
            group = jnp.where((t >= 0) & (rel >= 0), rel // LANES, 99)
            one = jnp.where(j_col == group, k_row, 0.0).astype(jnp.bfloat16)
            two = jnp.where(o_col == t % LANES, 1.0, 0.0).astype(jnp.bfloat16)
            found = lax.dot_general(one, two, (((1,), (1,)), ((), ())), preferred_element_type=jnp.float32).astype(jnp.int32)
            codes[:, p, :] = jnp.where(found > 0, p * K + found - 1, BIG)
        lane = lax.broadcasted_iota(jnp.int32, (32, LANES), 1)
        row = lax.broadcasted_iota(jnp.int32, (32, LANES), 0)
        sheet[...] = jnp.zeros_like(sheet)
        last = jnp.full((1, LANES), -1, jnp.int32)
        for slot in range(LIMIT):
            low = jnp.full((32, LANES), BIG, jnp.int32)
            for j in range(15):
                code = codes[j]
                low = jnp.minimum(low, jnp.where(code > last, code, BIG))
            low = jnp.min(low, axis=0, keepdims=True)
            key = jnp.zeros((32, LANES), jnp.int32)
            for j in range(15):
                hit = (codes[j] == low) & (low < BIG)
                key = key + jnp.where(hit, (32 * b + row) * VOCAB_PADDED + start + j * LANES + lane + 1, 0)
            sheet[8 + slot:9 + slot, :] = (jnp.sum(key, axis=0, keepdims=True) - 1).astype(jnp.float32)
            lows[slot:slot + 1, :] = low
            last = low

    back = (0, 2, 1, 3)

    def pool(slots):
        for r in range(4):
            for h in range(2):
                row = 2 * ((z + DELTA[r] + 4) % 4) + h
                for cc in range(2):
                    if r == 0:
                        parts = ((cc, 2 * h), (cc, 2 * h + 1))
                    elif r == 3:
                        parts = ((6 + h, 2 * cc), (6 + h, 2 * cc + 1))
                    else:
                        parts = ((2 + 2 * h, 2 * cc + r - 1), (3 + 2 * h, 2 * cc + r - 1))
                    for m in range(8):
                        slot = (0, 0, 1, 1, 1, 1, 3, 3)[m]
                        if slot not in slots:
                            continue
                        (k0, g0), (k1, g1) = parts
                        best = jnp.max(jnp.maximum(tops[m, k0, g0], tops[m, k1, g1]), axis=0, keepdims=True)
                        if slot == 1:
                            for i in range(2):
                                pooled[1 + i, cc, pl.ds(row, 1), 256 * (m - 2):256 * (m - 1)] = best[:, 256 * i:256 * i + 256]
                        else:
                            pooled[slot, cc, pl.ds(row, 1), PIECE * (m % 2):PIECE * (m % 2) + PIECE] = best

    def swap(slot):
        for cc in range(2):
            if (slot, cc) != (0, 0):
                send(("e", slot, cc), pooled.at[slot, cc], landed.at[cc, back[slot]], device(dx=DELTA[slot], flip=cc))

    def early():
        pool((0, 1))
        for slot in (1, 2, 0):
            swap(slot)

    acts = {
        "own_s": send_own_s, "own_w": send_own_w, "pair": pair_s, "rows": paired_s, "far": fwd_s,
        "share": share_w, "relay": relay_w, "columns": ready_w, "across": fwd_w, "codes": find_codes, "early": early,
    }

    def handle(todo):
        for name, *values in todo:
            acts[name](*values)

    def multiply(k, m):
        d = jnp.dot(states[k], weights[m], preferred_element_type=jnp.float32)
        tops[m, k] = jnp.max(d.reshape(4, 16, 8, PIECE), axis=1)

    def straight(table):
        for todo, pairs in table:
            handle(todo)
            for k, m in pairs:
                multiply(k, m)

    def looped(table):
        def step(n, _):
            for at, (todo, _) in enumerate(table):
                pl.when(n == at)(lambda: handle(todo))
            for part in range(len(table[0][1])):
                k, m = (
                    sum(jnp.where(n == at, pairs[part][i], 0) for at, (_, pairs) in enumerate(table) if pairs[part][i])
                    for i in range(2)
                )
                multiply(k, m)
            return 0

        lax.fori_loop(0, len(table), step, 0)

    straight(FIRST)
    looped(FOURS)
    looped(EIGHTS)
    straight(LAST)
    pool((3,))
    swap(3)
    landed[0, 0] = pooled[0, 0]

    def shape_of(name, width):
        if name[0] in ("x", "xf"):
            return weights.at[2, pl.ds(0, DIRECT[name[2]] if name[1] else SLICE[name[2]]), pl.ds(0, width)]
        if name[0] in ("y", "yf"):
            return weights.at[2, pl.ds(0, SLICE[dict((at, j) for j, at in strips(name[1]))[name[2]]]), pl.ds(0, width)]
        return {
            "z": states.at[0, pl.ds(0, 128)],
            "zf": states.at[0, pl.ds(0, 128)],
            "d": states.at[0] if name[1] == 1 else states.at[0, pl.ds(0, 256)],
            "e": pooled.at[0, 0],
            "pb": boxes.at[0],
            "pv": vocab_out.at[0],
        }[name[0]]

    def quarter_of(name):
        if name[0] in ("x", "xf"):
            return name[2]
        if name[0] in ("y", "yf"):
            return dict((at, j) for j, at in strips(name[1]))[name[2]]
        return 1

    def leave(name):
        by_core(quarter_of(name), lambda first, width: copy(name, shape_of(name, width), shape_of(name, width), device(flip=1)).wait_send())

    for name in [name for name in started if name[0] != "e"]:
        leave(name)
        started.remove(name)
    bias = vbias_ref[...].astype(jnp.float32).reshape(1, -1)
    columns = BLOCK * v + lax.broadcasted_iota(jnp.int32, (8, BLOCK), 1)
    for slot in (0, 1, 2, 3):
        for cc in range(2):
            if (slot, cc) != (0, 0):
                got(("e", back[slot], cc), landed.at[cc, slot])
        raw = jnp.concatenate([landed[c, slot], landed[1 - c, slot][:, 2 * WIDE - BLOCK:]], axis=1) + bias
        done = jnp.where(columns < VOCAB, jnp.log1p(jnp.maximum(raw, 0.0)), 0.0)
        vec[pl.ds(pl.multiple_of(8 * ((x + DELTA[slot] + 4) % 4), 8), 8), :] = done

    for slot in range(LIMIT):
        low = lows[slot:slot + 1, :]
        weight = jnp.zeros((32, LANES), jnp.float32)
        for j in range(15):
            hit = (codes[j] == low) & (low < BIG)
            weight = weight + jnp.where(hit, vec[:, j * LANES:(j + 1) * LANES], 0.0)
        sheet[slot:slot + 1, :] = jnp.sum(weight, axis=0, keepdims=True)
    store = pltpu.make_async_copy(vec, out_ref, local_sem.at[4])
    store.start()
    boxes[...] = jnp.transpose(sheet[...]).reshape(8, 16, LANES)
    for d in range(1, 8):
        to = (b + d) % 8
        send(("pb", d), boxes.at[to], batch_in.at[b], (to, v))
    batch_in[b] = boxes[b]
    for d in range(1, 8):
        got(("pb", d), batch_in.at[(b - d + 8) % 8])
    for origin in range(8):
        vocab_out[:, origin, :] = batch_in[origin]
    for d in range(1, 16):
        to = (v + d) % 16
        send(("pv", d), vocab_out.at[to], sheet_out_ref.at[v], (b, to))
    sheet_out_ref[v] = vocab_out[v]
    for d in range(1, 16):
        got(("pv", d), sheet_out_ref.at[(v - d + 16) % 16])

    store.wait()
    for name in started:
        leave(name)


MESSAGES = 112


def encode(hidden, dense_w, dense_b, norm_gain, norm_bias, vocabulary_weight, vocabulary_bias, lengths, term_ids):
    anywhere = pl.BlockSpec(memory_space=pl.ANY)
    vmem = pl.BlockSpec(memory_space=pltpu.VMEM)
    smem = pl.BlockSpec(memory_space=pltpu.SMEM)
    return pl.pallas_call(
        encode_kernel,
        in_specs=[smem, anywhere, anywhere, vmem, vmem, vmem, anywhere, vmem, vmem],
        out_specs=[anywhere, vmem],
        out_shape=[
            jax.ShapeDtypeStruct((32, BLOCK), jnp.float32),
            jax.ShapeDtypeStruct((16, 8, LANES), jnp.float32),
        ],
        scratch_shapes=[
            pltpu.VMEM((512, 768), jnp.bfloat16),
            pltpu.VMEM((768, 768), jnp.bfloat16),
            pltpu.VMEM((8, 512, 768), jnp.bfloat16),
            pltpu.VMEM((8, 768, PIECE), jnp.bfloat16),
            pltpu.VMEM((8, 8, 4, 8, PIECE), jnp.float32),
            pltpu.VMEM((4, 2, 8, WIDE), jnp.float32),
            pltpu.VMEM((2, 4, 8, WIDE), jnp.float32),
            pltpu.VMEM((16, 32, LANES), jnp.int32),
            pltpu.VMEM((8, LANES), jnp.int32),
            pltpu.VMEM((LANES, LANES), jnp.float32),
            pltpu.VMEM((8, 16, LANES), jnp.float32),
            pltpu.VMEM((8, 16, LANES), jnp.float32),
            pltpu.VMEM((16, 8, LANES), jnp.float32),
            pltpu.VMEM((32, BLOCK), jnp.float32),
            pltpu.SemaphoreType.DMA((5,)),
            pltpu.SemaphoreType.DMA((MESSAGES,)),
            pltpu.SemaphoreType.DMA((MESSAGES,)),
        ],
        compiler_params=pltpu.CompilerParams(collective_id=0, has_side_effects=True, vmem_limit_bytes=56 * 2**20),
    )(lengths, hidden, dense_w, dense_b, norm_gain, norm_bias, vocabulary_weight, vocabulary_bias, term_ids)


def finish_kernel(vectors_ref, sheet_ref, out_ref, out_w_ref, out_k_ref, rows):
    out_ref[...] = vectors_ref[...]
    for origin in range(16):
        rows[:, origin, :] = sheet_ref[origin]
    result = jnp.transpose(rows[...].reshape(LANES, LANES))
    out_w_ref[:, 0, :] = result[0:LIMIT]
    out_k_ref[:, 0, :] = result[8:8 + LIMIT].astype(jnp.int32)


def finish(vectors, sheet):
    vmem = pl.BlockSpec(memory_space=pltpu.VMEM)
    return pl.pallas_call(
        finish_kernel,
        in_specs=[vmem, vmem],
        out_specs=[vmem, vmem, vmem],
        out_shape=[
            jax.ShapeDtypeStruct(vectors.shape, jnp.float32),
            jax.ShapeDtypeStruct((LIMIT, 1, LANES), jnp.float32),
            jax.ShapeDtypeStruct((LIMIT, 1, LANES), jnp.int32),
        ],
        scratch_shapes=[pltpu.VMEM((8, 16, LANES), jnp.float32)],
    )(vectors, sheet)


def local(hidden, dense_w, dense_b, norm_gain, norm_bias, vocabulary_weight, vocabulary_bias, lengths, term_ids):
    vectors, sheet = encode(
        hidden, dense_w, dense_b, norm_gain, norm_bias, vocabulary_weight, vocabulary_bias, lengths, term_ids
    )
    vectors, weights, keys = finish(vectors, sheet)
    return vectors, jnp.swapaxes(weights, 0, 1), jnp.swapaxes(keys, 0, 1)


def solution(mesh):
    in_specs = (
        P(("batch", "vocab"), None), P(), P(), P(), P(),
        P(None, "vocab"), P("vocab"), P("batch"), P("batch", None),
    )
    out_specs = (P("batch", "vocab"), P(("batch", "vocab"), None, None), P(("batch", "vocab"), None, None))
    return jax.shard_map(local, mesh=mesh, in_specs=in_specs, out_specs=out_specs, check_vma=False)
```

time: 76.9 us -> 69.7 us (0.906)
  local copies, waits for them, and re-layouts: 5.46 us -> 0 us
  Pallas kernels: 70.5 us -> 68.8 us
    unnamed x3 -> x0, local copies, waits for them, and re-layouts: 4.17 us -> none
    pallas_call x1, Pallas kernels: 70.5 us -> 67.1 us  [encode(): pl.pallas_call(encode_kernel, in_specs=[smem, anywhere, anywhere, vmem, v...]
    pallas_call x0 -> x1, Pallas kernels: none -> 1.72 us  [finish(): pl.pallas_call(finish_kernel, in_specs=[vmem, vmem], out_specs=[vmem, vme...]
    broadcast_in_dim x1 -> x0, local copies, waits for them, and re-layouts: 1.29 us -> none  [local(): vocabulary_bias[None]]
where the time goes in v4:
time: 69.7 us; the launch traced here: 69.5 us
  Pallas kernels  68.8 us (99%)
    pallas_call x1, Pallas kernels, encode(): pl.pallas_call(encode_kernel, in_specs=[smem, anywhere, anywhere, vmem, v...  67.1 us
    pallas_call x1, Pallas kernels, finish(): pl.pallas_call(finish_kernel, in_specs=[vmem, vmem], out_specs=[vmem, vme...  1.72 us

profile of v4, /device:TPU:1, one launch (start us, length us, event | category | flops | bytes accessed | tf_op | source)
XLA Modules:
  0.0 69.5 jit_solution(2295317277186882917)
XLA Ops:
  0.6 67.1 %shard_map.112 = (f32[32,1920]{1,0:T(8,128)}, f32[16,8,128]{2,1,0:T(8,128)}) custom-call(s32[32]{0:T(128)} %lengths_ref.1, bf16[512,768]{1,0:T(8,128)(2,1)} %hidden_ref.1, bf16[768,768]{1,0:T(8,128)(2,1)} %dense_ref.1, f32[768]{0:T(1024)} %b_ref.1, f32[768]{0:T(1024)} %gain_ref.1, f32[768]{0:T(1024)} %bias_ref.1, bf16[768,1920]{1,0:T(8,128)(2,1)} %weight_ref.1, ...), custom_call_target="tpu_custom_call" | custom-call | tf_op jit(solution)/shard_map/pallas_call | solution.py:439
  67.7 1.7 %shard_map.113 = (f32[32,1920]{1,0:T(8,128)}, f32[5,1,128]{2,1,0:T(1,128)}, s32[5,1,128]{2,1,0:T(1,128)}) custom-call(f32[32,1920]{1,0:T(8,128)} %get-tuple-element.8.vectors_ref, f32[16,8,128]{2,1,0:T(8,128)} %get-tuple-element.9.sheet_ref), custom_call_target="tpu_custom_call" | custom-call | tf_op jit(solution)/shard_map/pallas_call | solution.py:481

commit v5 on v4

--- a/solution.py
+++ b/solution.py
@@ -15,7 +15,7 @@
 BLOCK = 1920
 WIDE = 1024
 PIECE = 512
-DIRECT = (640, 256, 256, 256)
+DIRECT = (512, 320, 384, 320)
 SLICE = tuple((768 - rows) // 4 for rows in DIRECT)
 DELTA = (0, -1, 1, 2)
 
@@ -25,21 +25,24 @@
 )
 FOURS = (
     (
-        (("across", 0, 0), ("own_w", 1, 2), ("codes",), ("relay", 2), ("pair", 2), ("rows", 2), ("relay", 3), ("columns", 2)),
+        (
+            ("across", 0, 0), ("own_w", 1, 2), ("codes",), ("relay", 2), ("pair", 2), ("rows", 2), ("relay", 3), ("columns", 2),
+            ("pair", 3), ("share", 4),
+        ),
         ((0, 2), (1, 2), (2, 0), (2, 1)),
     ),
-    ((("share", 4), ("pair", 3), ("far", 0), ("rows", 3)), ((2, 2), (3, 0), (3, 1), (3, 2))),
+    ((("share", 5), ("far", 0), ("rows", 3)), ((2, 2), (3, 0), (3, 1), (3, 2))),
     (
-        (("share", 5), ("across", 0, 1), ("own_w", 1, 3), ("pair", 4), ("columns", 3)),
+        (("across", 0, 1), ("own_w", 1, 3), ("pair", 4), ("columns", 3), ("relay", 4)),
         ((0, 3), (1, 3), (2, 3), (3, 3)),
     ),
-    ((("across", 1, 0), ("relay", 4), ("rows", 4)), ((4, 0), (4, 1), (4, 2), (4, 3))),
-    ((("pair", 5), ("far", 1), ("relay", 5), ("share", 6), ("columns", 4)), ((0, 4), (1, 4), (2, 4), (3, 4))),
-    ((("share", 7), ("across", 1, 1), ("rows", 5)), ((4, 4), (5, 0), (5, 1), (5, 2))),
+    ((("across", 1, 0), ("rows", 4), ("relay", 5)), ((4, 0), (4, 1), (4, 2), (4, 3))),
+    ((("pair", 5), ("far", 1), ("share", 6), ("columns", 4)), ((0, 4), (1, 4), (2, 4), (3, 4))),
+    ((("share", 7), ("rows", 5)), ((4, 4), (5, 0), (5, 1), (5, 2))),
 )
 EIGHTS = (
     (
-        (("relay", 6), ("columns", 5), ("pair", 6)),
+        (("across", 1, 1), ("relay", 6), ("columns", 5), ("pair", 6)),
         ((5, 3), (5, 4), (0, 5), (1, 5), (2, 5), (3, 5), (4, 5), (5, 5)),
     ),
     (
@@ -370,10 +373,10 @@
         return {
             "z": states.at[0, pl.ds(0, 128)],
             "zf": states.at[0, pl.ds(0, 128)],
-            "d": states.at[0] if name[1] == 1 else states.at[0, pl.ds(0, 256)],
+            "d": states.at[0] if name[-1] == 1 else states.at[0, pl.ds(0, 256)],
             "e": pooled.at[0, 0],
-            "pb": boxes.at[0],
-            "pv": vocab_out.at[0],
+            "pb": boxes.at[pl.ds(0, 7)],
+            "pv": vocab_out.at[pl.ds(0, 15)],
         }[name[0]]
 
     def quarter_of(name):
@@ -411,25 +414,25 @@
     boxes[...] = jnp.transpose(sheet[...]).reshape(8, 16, LANES)
     for d in range(1, 8):
         to = (b + d) % 8
-        send(("pb", d), boxes.at[to], batch_in.at[b], (to, v))
+        send(("pb",), boxes.at[to], batch_in.at[b], (to, v))
     batch_in[b] = boxes[b]
-    for d in range(1, 8):
-        got(("pb", d), batch_in.at[(b - d + 8) % 8])
+    got(("pb",), batch_in.at[pl.ds(0, 7)])
     for origin in range(8):
         vocab_out[:, origin, :] = batch_in[origin]
     for d in range(1, 16):
         to = (v + d) % 16
-        send(("pv", d), vocab_out.at[to], sheet_out_ref.at[v], (b, to))
-    sheet_out_ref[v] = vocab_out[v]
-    for d in range(1, 16):
-        got(("pv", d), sheet_out_ref.at[(v - d + 16) % 16])
+        send(("pv",), vocab_out.at[to], sheet_out_ref.at[v], (b, to))
+    keep = pltpu.make_async_copy(vocab_out.at[v], sheet_out_ref.at[v], local_sem.at[5])
+    keep.start()
+    got(("pv",), sheet_out_ref.at[pl.ds(0, 15)])
 
     store.wait()
+    keep.wait()
     for name in started:
         leave(name)
 
 
-MESSAGES = 112
+MESSAGES = 89
 
 
 def encode(hidden, dense_w, dense_b, norm_gain, norm_bias, vocabulary_weight, vocabulary_bias, lengths, term_ids):
@@ -439,7 +442,7 @@
     return pl.pallas_call(
         encode_kernel,
         in_specs=[smem, anywhere, anywhere, vmem, vmem, vmem, anywhere, vmem, vmem],
-        out_specs=[anywhere, vmem],
+        out_specs=[anywhere, anywhere],
         out_shape=[
             jax.ShapeDtypeStruct((32, BLOCK), jnp.float32),
             jax.ShapeDtypeStruct((16, 8, LANES), jnp.float32),
@@ -459,7 +462,7 @@
             pltpu.VMEM((8, 16, LANES), jnp.float32),
             pltpu.VMEM((16, 8, LANES), jnp.float32),
             pltpu.VMEM((32, BLOCK), jnp.float32),
-            pltpu.SemaphoreType.DMA((5,)),
+            pltpu.SemaphoreType.DMA((6,)),
             pltpu.SemaphoreType.DMA((MESSAGES,)),
             pltpu.SemaphoreType.DMA((MESSAGES,)),
         ],

time: 69.7 us -> 66.2 us (0.950)
  Pallas kernels: 68.8 us -> 65.3 us
    pallas_call x1, Pallas kernels: 67.1 us -> 63.6 us  [encode(): pl.pallas_call(encode_kernel, in_specs=[smem, anywhere, anywhere, vmem, v...]
where the time goes in v5:
time: 66.2 us; the launch traced here: 66 us
  Pallas kernels  65.3 us (99%)
    pallas_call x1, Pallas kernels, encode(): pl.pallas_call(encode_kernel, in_specs=[smem, anywhere, anywhere, vmem, v...  63.6 us
    pallas_call x1, Pallas kernels, finish(): pl.pallas_call(finish_kernel, in_specs=[vmem, vmem], out_specs=[vmem, vme...  1.72 us

profile of v5, /device:TPU:1, one launch (start us, length us, event | category | flops | bytes accessed | tf_op | source)
XLA Modules:
  0.0 66.0 jit_solution(15178550903315220488)
XLA Ops:
  0.6 63.6 %shard_map.112 = (f32[32,1920]{1,0:T(8,128)}, f32[16,8,128]{2,1,0:T(8,128)}) custom-call(s32[32]{0:T(128)} %lengths_ref.1, bf16[512,768]{1,0:T(8,128)(2,1)} %hidden_ref.1, bf16[768,768]{1,0:T(8,128)(2,1)} %dense_ref.1, f32[768]{0:T(1024)} %b_ref.1, f32[768]{0:T(1024)} %gain_ref.1, f32[768]{0:T(1024)} %bias_ref.1, bf16[768,1920]{1,0:T(8,128)(2,1)} %weight_ref.1, ...), custom_call_target="tpu_custom_call" | custom-call | tf_op jit(solution)/shard_map/pallas_call | solution.py:442
  64.2 1.7 %shard_map.113 = (f32[32,1920]{1,0:T(8,128)}, f32[5,1,128]{2,1,0:T(1,128)}, s32[5,1,128]{2,1,0:T(1,128)}) custom-call(f32[32,1920]{1,0:T(8,128)} %get-tuple-element.8.vectors_ref, f32[16,8,128]{2,1,0:T(8,128)} %get-tuple-element.9.sheet_ref), custom_call_target="tpu_custom_call" | custom-call | tf_op jit(solution)/shard_map/pallas_call | solution.py:484

commit v6 on v5

--- a/solution.py
+++ b/solution.py
@@ -74,7 +74,16 @@
     x, z = v // 4, v % 4
     sign = 1 - 2 * c
     number = Numbers()
-    started = []
+
+    def group_of(name):
+        if name[0] in ("x", "xf"):
+            quarter = name[2]
+        elif name[0] in ("y", "yf"):
+            quarter = name[1] - 2 if name[1] < 6 else 2 * name[1] - 12 + name[2] // 256
+        else:
+            return {"z": 0, "zf": 0, "d": 0, "e": 3, "pb": 4, "pv": 5}[name[0]]
+        return 2 if quarter else 1
+
 
     def device(dx=0, dy=0, dz=0, flip=0):
         core = 1 - c if flip else c
@@ -84,14 +93,12 @@
         i = number(*name)
         assert i < MESSAGES
         return pltpu.make_async_remote_copy(
-            src_ref=source, dst_ref=target, send_sem=send_sem.at[i], recv_sem=recv_sem.at[i],
+            src_ref=source, dst_ref=target, send_sem=send_sem.at[group_of(name)], recv_sem=recv_sem.at[i],
             device_id=to, device_id_type=MESH,
         )
 
     def send(name, source, target, to):
         copy(name, source, target, to).start()
-        if name not in started:
-            started.append(name)
 
     waited = []
 
@@ -137,7 +144,7 @@
         def act(first, width):
             for side, dx in ((0, 1), (1, -1)):
                 send(
-                    ("x", kind, j, side),
+                    ("x", kind, j),
                     weights.at[j // 2, kind_rows(kind, j), pl.ds(256 * (j % 2) + first, width)],
                     weights.at[2 + j, kind_rows(kind, j), pl.ds(256 * side + first, width)],
                     device(dx=dx),
@@ -147,8 +154,7 @@
 
     def got_own_w(kind, j):
         def act(first, width):
-            for side in range(2):
-                got(("x", kind, j, side), weights.at[2 + j, kind_rows(kind, j), pl.ds(256 * side + first, width)])
+            got(("x", kind, j), weights.at[2 + j, kind_rows(kind, j), pl.ds(0, 2 * width)])
 
         once(("x", kind, j), lambda: by_core(j, act))
 
@@ -176,33 +182,35 @@
             def act(first, width):
                 piece = weights.at[m, y_rows(j, 0), pl.ds(at + first, width)]
                 for side, dy in ((0, 1), (1, -1)):
-                    send(("y", m, at, side), piece, piece, device(dy=dy))
+                    send(("y", m, at if m >= 6 else 0), piece, piece, device(dy=dy))
 
             by_core(j, act)
 
+    def together(m):
+        return ((m - 2, 0, 2),) if m < 6 else ((2 * m - 12, 0, 1), (2 * m - 11, 256, 1))
+
     def relay_w(m):
+        for j, at, n in together(m):
+            by_core(j, lambda first, width: got(("y", m, at), weights.at[m, pl.ds(0, 2 * SLICE[j]), pl.ds(at, n * width)]))
         for j, at in strips(m):
             def act(first, width):
-                got(("y", m, at, 0), weights.at[m, y_rows(j, -1), pl.ds(at + first, width)])
-                got(("y", m, at, 1), weights.at[m, y_rows(j, 1), pl.ds(at + first, width)])
                 piece = weights.at[m, y_rows(j, -sign), pl.ds(at + first, width)]
-                send(("yf", m, at), piece, piece, device(dy=sign))
+                send(("yf", m, at if m >= 6 else 0), piece, piece, device(dy=sign))
 
             by_core(j, act)
 
     def ready_w(m):
-        for j, at in strips(m):
-            by_core(j, lambda first, width: got(("yf", m, at), weights.at[m, y_rows(j, 2), pl.ds(at + first, width)]))
+        for j, at, n in together(m):
+            by_core(j, lambda first, width: got(("yf", m, at), weights.at[m, pl.ds(0, SLICE[j]), pl.ds(at, n * width)]))
         got_own_w(1, m - 2) if m < 6 else got_fwd_w(1, m - 6)
 
     def send_own_s(q):
         for side, dz in ((0, 1), (1, -1)):
-            send(("z", q, side), states.at[0, pl.ds(128 * q, 128)], states.at[2 + q, pl.ds(128 * side, 128)], device(dz=dz))
+            send(("z", q), states.at[0, pl.ds(128 * q, 128)], states.at[2 + q, pl.ds(128 * side, 128)], device(dz=dz))
 
     def got_own_s(q):
         def act():
-            for side in range(2):
-                got(("z", q, side), states.at[2 + q, pl.ds(128 * side, 128)])
+            got(("z", q), states.at[2 + q, pl.ds(0, 256)])
 
         once(("z", q), act)
 
@@ -210,11 +218,10 @@
         for q in (2 * h, 2 * h + 1):
             got_own_s(q)
             source = states.at[2 + q, pl.ds(pl.multiple_of(128 * c, 128), 128)]
-            send(("zf", q), source, states.at[6 + h, pl.ds(128 * (q % 2), 128)], device(dz=sign))
+            send(("zf", h), source, states.at[6 + h, pl.ds(128 * (q % 2), 128)], device(dz=sign))
 
     def got_fwd_s(h):
-        for q in (2 * h, 2 * h + 1):
-            got(("zf", q), states.at[6 + h, pl.ds(128 * (q % 2), 128)])
+        got(("zf", h), states.at[6 + h, pl.ds(0, 256)])
 
     def pair_s(k):
         if k >= 6:
@@ -365,33 +372,12 @@
     swap(3)
     landed[0, 0] = pooled[0, 0]
 
-    def shape_of(name, width):
-        if name[0] in ("x", "xf"):
-            return weights.at[2, pl.ds(0, DIRECT[name[2]] if name[1] else SLICE[name[2]]), pl.ds(0, width)]
-        if name[0] in ("y", "yf"):
-            return weights.at[2, pl.ds(0, SLICE[dict((at, j) for j, at in strips(name[1]))[name[2]]]), pl.ds(0, width)]
-        return {
-            "z": states.at[0, pl.ds(0, 128)],
-            "zf": states.at[0, pl.ds(0, 128)],
-            "d": states.at[0] if name[-1] == 1 else states.at[0, pl.ds(0, 256)],
-            "e": pooled.at[0, 0],
-            "pb": boxes.at[pl.ds(0, 7)],
-            "pv": vocab_out.at[pl.ds(0, 15)],
-        }[name[0]]
-
-    def quarter_of(name):
-        if name[0] in ("x", "xf"):
-            return name[2]
-        if name[0] in ("y", "yf"):
-            return dict((at, j) for j, at in strips(name[1]))[name[2]]
-        return 1
-
-    def leave(name):
-        by_core(quarter_of(name), lambda first, width: copy(name, shape_of(name, width), shape_of(name, width), device(flip=1)).wait_send())
-
-    for name in [name for name in started if name[0] != "e"]:
-        leave(name)
-        started.remove(name)
+    def leave(name, region):
+        copy(name, region, region, device(flip=1)).wait_send()
+
+    leave(("z", 0), states.at[pl.ds(0, 7)])
+    by_core(0, lambda first, width: leave(("x", 0, 0), weights.at[pl.ds(0, 3), :, pl.ds(0, width)]))
+    leave(("x", 0, 1), weights.at[pl.ds(0, 6), :, pl.ds(0, 384)])
     bias = vbias_ref[...].astype(jnp.float32).reshape(1, -1)
     columns = BLOCK * v + lax.broadcasted_iota(jnp.int32, (8, BLOCK), 1)
     for slot in (0, 1, 2, 3):
@@ -428,11 +414,12 @@
 
     store.wait()
     keep.wait()
-    for name in started:
-        leave(name)
-
-
-MESSAGES = 89
+    leave(("e", 0, 1), tops.at[0, pl.ds(0, 7), pl.ds(0, 2)])
+    leave(("pb",), boxes.at[pl.ds(0, 7)])
+    leave(("pv",), vocab_out.at[pl.ds(0, 15)])
+
+
+MESSAGES = 54
 
 
 def encode(hidden, dense_w, dense_b, norm_gain, norm_bias, vocabulary_weight, vocabulary_bias, lengths, term_ids):
@@ -463,7 +450,7 @@
             pltpu.VMEM((16, 8, LANES), jnp.float32),
             pltpu.VMEM((32, BLOCK), jnp.float32),
             pltpu.SemaphoreType.DMA((6,)),
-            pltpu.SemaphoreType.DMA((MESSAGES,)),
+            pltpu.SemaphoreType.DMA((6,)),
             pltpu.SemaphoreType.DMA((MESSAGES,)),
         ],
         compiler_params=pltpu.CompilerParams(collective_id=0, has_side_effects=True, vmem_limit_bytes=56 * 2**20),

time: 66.2 us -> 65.7 us (level)
  no operation moved by 1% of the time
where the time goes in v6:
time: 65.7 us; the launch traced here: 65.5 us
  Pallas kernels  64.9 us (99%)
    pallas_call x1, Pallas kernels, encode(): pl.pallas_call(encode_kernel, in_specs=[smem, anywhere, anywhere, vmem, v...  63.1 us
    pallas_call x1, Pallas kernels, finish(): pl.pallas_call(finish_kernel, in_specs=[vmem, vmem], out_specs=[vmem, vme...  1.72 us

profile of v6, /device:TPU:1, one launch (start us, length us, event | category | flops | bytes accessed | tf_op | source)
XLA Modules:
  0.0 65.5 jit_solution(5458318578547029717)
XLA Ops:
  0.6 63.1 %shard_map.112 = (f32[32,1920]{1,0:T(8,128)}, f32[16,8,128]{2,1,0:T(8,128)}) custom-call(s32[32]{0:T(128)} %lengths_ref.1, bf16[512,768]{1,0:T(8,128)(2,1)} %hidden_ref.1, bf16[768,768]{1,0:T(8,128)(2,1)} %dense_ref.1, f32[768]{0:T(1024)} %b_ref.1, f32[768]{0:T(1024)} %gain_ref.1, f32[768]{0:T(1024)} %bias_ref.1, bf16[768,1920]{1,0:T(8,128)(2,1)} %weight_ref.1, ...), custom_call_target="tpu_custom_call" | custom-call | tf_op jit(solution)/shard_map/pallas_call | solution.py:429
  63.8 1.7 %shard_map.113 = (f32[32,1920]{1,0:T(8,128)}, f32[5,1,128]{2,1,0:T(1,128)}, s32[5,1,128]{2,1,0:T(1,128)}) custom-call(f32[32,1920]{1,0:T(8,128)} %get-tuple-element.8.vectors_ref, f32[16,8,128]{2,1,0:T(8,128)} %get-tuple-element.9.sheet_ref), custom_call_target="tpu_custom_call" | custom-call | tf_op jit(solution)/shard_map/pallas_call | solution.py:471

commit v7 on v6

--- a/solution.py
+++ b/solution.py
@@ -64,9 +64,9 @@
 
 
 def encode_kernel(
-    lengths_ref, hidden_ref, dense_ref, b_ref, gain_ref, bias_ref, weight_ref, vbias_ref, terms_ref,
+    lengths_ref, hidden_ref, dense_ref, b_ref, gain_ref, bias_ref, weight_ref, vbias_ref, terms_hbm_ref,
     out_ref, sheet_out_ref,
-    hid, den, states, weights, tops, pooled, landed, codes, lows, sheet, boxes, batch_in, vocab_out, vec,
+    hid, den, states, weights, tops, pooled, landed, codes, lows, sheet, boxes, batch_in, vocab_out, vec, terms_ref,
     local_sem, send_sem, recv_sem,
 ):
     b, v = lax.axis_index("batch"), lax.axis_index("vocab")
@@ -134,6 +134,8 @@
     load_h.start()
     for load in load_w:
         load.start()
+    load_t = pltpu.make_async_copy(terms_hbm_ref, terms_ref, local_sem.at[6])
+    load_t.start()
     barrier = pltpu.get_barrier_semaphore()
     friends = [((b + d) % 8, v) for d in range(1, 8)] + [(b, (v + d) % 16) for d in range(1, 16)]
     friends += [device(dx, 0, 0, 1) for dx in range(1, 4)]
@@ -266,6 +268,7 @@
             send_own_s(q - 1)
 
     def find_codes():
+        load_t.wait()
         k_row = (lax.broadcasted_iota(jnp.int32, (1, K), 1) + 1).astype(jnp.float32)
         j_col = lax.broadcasted_iota(jnp.int32, (16, K), 0)
         o_col = lax.broadcasted_iota(jnp.int32, (LANES, K), 0)
@@ -428,7 +431,7 @@
     smem = pl.BlockSpec(memory_space=pltpu.SMEM)
     return pl.pallas_call(
         encode_kernel,
-        in_specs=[smem, anywhere, anywhere, vmem, vmem, vmem, anywhere, vmem, vmem],
+        in_specs=[smem, anywhere, anywhere, vmem, vmem, vmem, anywhere, vmem, anywhere],
         out_specs=[anywhere, anywhere],
         out_shape=[
             jax.ShapeDtypeStruct((32, BLOCK), jnp.float32),
@@ -449,7 +452,8 @@
             pltpu.VMEM((8, 16, LANES), jnp.float32),
             pltpu.VMEM((16, 8, LANES), jnp.float32),
             pltpu.VMEM((32, BLOCK), jnp.float32),
-            pltpu.SemaphoreType.DMA((6,)),
+            pltpu.VMEM((32, K), jnp.int32),
+            pltpu.SemaphoreType.DMA((7,)),
             pltpu.SemaphoreType.DMA((6,)),
             pltpu.SemaphoreType.DMA((MESSAGES,)),
         ],

time: 65.7 us -> 65.7 us (level)
  no operation moved by 1% of the time
where the time goes in v7:
time: 65.7 us; the launch traced here: 65.5 us
  Pallas kernels  64.9 us (99%)
    pallas_call x1, Pallas kernels, encode(): pl.pallas_call(encode_kernel, in_specs=[smem, anywhere, anywhere, vmem, v...  63.1 us
    pallas_call x1, Pallas kernels, finish(): pl.pallas_call(finish_kernel, in_specs=[vmem, vmem], out_specs=[vmem, vme...  1.72 us

profile of v7, /device:TPU:1, one launch (start us, length us, event | category | flops | bytes accessed | tf_op | source)
XLA Modules:
  0.0 65.5 jit_solution(14368797125101238000)
XLA Ops:
  0.6 63.1 %shard_map.112 = (f32[32,1920]{1,0:T(8,128)}, f32[16,8,128]{2,1,0:T(8,128)}) custom-call(s32[32]{0:T(128)} %lengths_ref.1, bf16[512,768]{1,0:T(8,128)(2,1)} %hidden_ref.1, bf16[768,768]{1,0:T(8,128)(2,1)} %dense_ref.1, f32[768]{0:T(1024)} %b_ref.1, f32[768]{0:T(1024)} %gain_ref.1, f32[768]{0:T(1024)} %bias_ref.1, bf16[768,1920]{1,0:T(8,128)(2,1)} %weight_ref.1, ...), custom_call_target="tpu_custom_call" | custom-call | tf_op jit(solution)/shard_map/pallas_call | solution.py:432
  63.8 1.7 %shard_map.113 = (f32[32,1920]{1,0:T(8,128)}, f32[5,1,128]{2,1,0:T(1,128)}, s32[5,1,128]{2,1,0:T(1,128)}) custom-call(f32[32,1920]{1,0:T(8,128)} %get-tuple-element.8.vectors_ref, f32[16,8,128]{2,1,0:T(8,128)} %get-tuple-element.9.sheet_ref), custom_call_target="tpu_custom_call" | custom-call | tf_op jit(solution)/shard_map/pallas_call | solution.py:475
